TPU v7x, 256 devices: a whole 4x4x8 slice. The times are simulated.
256 devices in a mesh: group: 2 (over z_lo), row: 8 (over y, core), col: 16 (over z_hi, x).
Axes of the slice: x: 4, y: 4, z: 8 (z_hi: 4, z_lo: 2; z = z_hi * 2 + z_lo), core: 2. Of those that a mesh axis runs over, the one named last changes fastest.
Arguments:
- pair_repr: bfloat16 [256, 256, 128], P(('group', 'row'), 'col'), may hold values from -6 to 6
- pair_mask: int32 [256, 256], P(('group', 'row'), 'col'), may hold values 0 or 1
- chain_id: int32 [256], replicated, may hold values from 0 to 7, never falling along the last dimension, each value on 1 to 64 neighbouring positions
- tri_in_gain: float32 [128], replicated, may hold values from 0.5 to 1.5
- tri_proj: bfloat16 [128, 512], replicated, may hold values from -0.5 to 0.5
- tri_gate: bfloat16 [128, 128], replicated, may hold values from -0.5 to 0.5
- tri_out_gain: float32 [128], replicated, may hold values from 0.5 to 1.5
- tri_out: bfloat16 [128, 128], replicated, may hold values from -0.5 to 0.5
- bias_gain: float32 [128], replicated, may hold values from 0.5 to 1.5
- bias_weight: bfloat16 [128, 16], replicated, may hold values from -0.5 to 0.5
- chain_bias: float32 [16], replicated, may hold values from -2 to 2
- tokens: bfloat16 [48, 256, 768], P(('group', 'row')), may hold values from -6 to 6
- noise_level: int32 [48], P(('group', 'row')), may hold values from 0 to 199
- attn_gain: float32 [768], replicated, may hold values from 0.5 to 1.5
- attn_weight: bfloat16 [4, 768, 768], P(None, None, 'col'), may hold values from -0.21875 to 0.21875
- out_weight: bfloat16 [768, 768], P('col'), may hold values from -0.21875 to 0.21875
- cotangent: bfloat16 [48, 256, 768], P(('group', 'row')), may hold values from -6 to 6
Outputs:
- pair_next: bfloat16 [256, 256, 128], P(('group', 'row'), 'col')
- pair_grad: float32 [256, 256, 128], P(('group', 'row'), 'col')
- bias_weight_grad: float32 [128, 16], replicated
- denoised: bfloat16 [48, 256, 768], P(('group', 'row'), 'col')
- token_grad: bfloat16 [48, 256, 768], P(('group', 'row'), 'col')
- attn_weight_grad: float32 [4, 768, 768], P(None, ('group', 'row'), 'col')
- out_weight_grad: float32 [768, 768], P('col', ('group', 'row'))
Inputs may be any that keep to these rules, and one draw needn't show every extreme that they name: `chain_id`: chain numbers never fall along the tokens.
All inputs are finite; a program needn't handle non-finite values. No bound on the sum of `pair_mask` on one device may be relied on, other than what follows from the above.
Results may differ from a plain program's by a relative error of at most 0.014.
Values may be sent and summed in bfloat16 or wider, within the bound.
A program may use at most 64 MiB of HBM per device.

v0:
```python
import functools
import math

import jax
import jax.numpy as jnp
from jax import lax
from jax.sharding import Mesh
from jax.sharding import PartitionSpec as P

LEVELS = 200
GROUP_ROW = ("group", "row_0", "row_1")
COL = ("col_0", "col_1")
GROUP_ROW_COL = ("group", "row_0", "row_1", "col_0", "col_1")


EPSILON = 1e-05
SIGMA_LOW = 0.1
SIGMA_SPAN = 100.0


def joined_along(parts, dim):
    shape = list(parts.shape[1:])
    shape[dim] *= parts.shape[0]
    return jnp.moveaxis(parts, 0, dim).reshape(shape)


def sent_to_all(array, axis):
    copies = jnp.broadcast_to(array, (lax.axis_size(axis), *array.shape))
    return lax.all_to_all(copies, axis, split_axis=0, concat_axis=0, tiled=True)


def collect(array, axis, dim):
    return joined_along(sent_to_all(array, axis), dim)


def split_up(array, dim, size):
    shape = array.shape
    parts = array.reshape(*shape[:dim], size, shape[dim] // size, *shape[dim + 1 :])
    return jnp.moveaxis(parts, dim, 0)


def summed_on_arrival(array, axis, dim):
    parts = split_up(array, dim, lax.axis_size(axis))
    arrived = lax.all_to_all(parts, axis, split_axis=0, concat_axis=0, tiled=True)
    return arrived.astype(jnp.float32).sum(axis=0)


def side_by_side(arrays, axis, dim, along):
    both = jnp.concatenate(arrays, axis=along)
    whole, at, done = (lax.psum_scatter(both, axis, scatter_dimension=dim, tiled=True), 0, [])
    for a in arrays:
        done.append(lax.slice_in_dim(whole, at, at + a.shape[along], axis=along))
        at += a.shape[along]
    return tuple(done)


def by_axis(array, axes):
    return functools.reduce(lax.psum, axes, array)


def normalize(values):
    average = jnp.mean(values, -1, keepdims=True)
    centred = values - average
    return centred * lax.rsqrt(jnp.mean(centred * centred, -1, keepdims=True) + EPSILON)


def norm_back(gradient, values, norm_gain):
    average = jnp.mean(values, -1, keepdims=True)
    centred = values - average
    inverse = lax.rsqrt(jnp.mean(centred * centred, -1, keepdims=True) + EPSILON)
    normed = centred * inverse
    weighted = gradient * norm_gain
    return inverse * (
        weighted
        - jnp.mean(weighted, -1, keepdims=True)
        - normed * jnp.mean(weighted * normed, -1, keepdims=True)
    )


def noise_scale(levels):
    sigma_vals = SIGMA_LOW * SIGMA_SPAN ** (levels.astype(jnp.float32) / (LEVELS - 1))
    return lax.rsqrt(1.0 + sigma_vals * sigma_vals)


def shards(
    pair_repr,
    pair_mask,
    chain_id,
    tri_in_gain,
    tri_proj,
    tri_gate,
    tri_out_gain,
    tri_out,
    bias_gain,
    bias_weight,
    chain_bias,
    tokens,
    noise_level,
    attn_gain,
    attn_weight,
    out_weight,
    cotangent,
):
    rows_here = pair_repr.shape[0]
    cols_here = pair_repr.shape[1]
    channels = pair_repr.shape[2]
    token_count = chain_id.shape[0]
    heads_all = bias_weight.shape[1]
    hidden_width = attn_gain.shape[0]
    head_size = hidden_width // heads_all
    inverse_square_root = 1.0 / math.sqrt(head_size)
    row_index = lax.axis_index(GROUP_ROW)
    col_index = lax.axis_index(COL)
    pair_tile = pair_repr.astype(jnp.float32)
    pair_in = (normalize(pair_tile) * tri_in_gain).astype(jnp.bfloat16)
    flat_in = pair_in.reshape(-1, channels)
    projected = jnp.dot(flat_in, tri_proj, preferred_element_type=jnp.float32).reshape(
        rows_here, cols_here, 4, channels
    )
    mask_tile = pair_mask.astype(jnp.float32)[:, :, None]
    left_proj = (jax.nn.sigmoid(projected[:, :, 0]) * projected[:, :, 1] * mask_tile).astype(
        jnp.bfloat16
    )
    right_proj = (jax.nn.sigmoid(projected[:, :, 2]) * projected[:, :, 3] * mask_tile).astype(
        jnp.bfloat16
    )
    gate_act = jax.nn.sigmoid(
        jnp.dot(flat_in, tri_gate, preferred_element_type=jnp.float32)
    ).reshape(rows_here, cols_here, channels)
    left_major = jnp.transpose(left_proj, (2, 0, 1))
    right_major = jnp.transpose(right_proj, (2, 0, 1))
    partial_rows = jnp.einsum(
        "cjk,cik->cji",
        collect(right_major, GROUP_ROW, 1),
        left_major,
        preferred_element_type=jnp.float32,
    )
    summed = summed_on_arrival(partial_rows.astype(jnp.bfloat16), COL, 1)
    triangle = jnp.transpose(summed, (2, 1, 0))
    tri_normed = (normalize(triangle) * tri_out_gain).astype(jnp.bfloat16)
    update = jnp.dot(
        tri_normed.reshape(-1, channels), tri_out, preferred_element_type=jnp.float32
    ).reshape(rows_here, cols_here, channels)
    updated = pair_tile + gate_act * update
    bias_in = (normalize(updated) * bias_gain).astype(jnp.bfloat16)
    flat_bias = bias_in.reshape(-1, channels)
    bias_tile = jnp.dot(flat_bias, bias_weight, preferred_element_type=jnp.float32).reshape(
        rows_here, cols_here, heads_all
    )
    row_chain = lax.dynamic_slice_in_dim(chain_id, row_index * rows_here, rows_here)
    col_chain = lax.dynamic_slice_in_dim(chain_id, col_index * cols_here, cols_here)
    same_chain = (row_chain[:, None] == col_chain[None, :]).astype(jnp.float32)
    bias_tile = bias_tile + same_chain[:, :, None] * chain_bias
    bias_major = jnp.transpose(bias_tile.astype(jnp.bfloat16), (2, 0, 1))
    head_rows = lax.all_to_all(bias_major, COL, split_axis=0, concat_axis=2, tiled=True)
    per_head_bias = collect(head_rows, GROUP_ROW, 1).astype(jnp.float32)
    local_heads = per_head_bias.shape[0]
    scales = noise_scale(noise_level)

    def one_copy(carried, inputs):
        bias_sums, weight_sums, output_sums = carried
        token_rows, cot_rows, scaling = inputs
        sequence_length = token_rows.shape[0]
        scaled = scaling * token_rows.astype(jnp.float32)
        hidden = (normalize(scaled) * attn_gain).astype(jnp.bfloat16)
        projections = jnp.einsum(
            "nd,gde->gne", hidden, attn_weight, preferred_element_type=jnp.float32
        )
        query_rows = (
            projections[0].astype(jnp.bfloat16).reshape(sequence_length, local_heads, head_size)
        )
        key_matrix = (
            projections[1].astype(jnp.bfloat16).reshape(sequence_length, local_heads, head_size)
        )
        value_rows = (
            projections[2].astype(jnp.bfloat16).reshape(sequence_length, local_heads, head_size)
        )
        gate_sig = jax.nn.sigmoid(projections[3])
        logit_scores = (
            jnp.einsum("fuc,suc->ufs", query_rows, key_matrix, preferred_element_type=jnp.float32)
            * inverse_square_root
            + per_head_bias
        )
        exponent = jnp.exp(logit_scores)
        attention = exponent / jnp.sum(exponent, -1, keepdims=True)
        attention_probs = attention.astype(jnp.bfloat16)
        attended_rows = jnp.einsum(
            "vkq,qvy->kvy", attention_probs, value_rows, preferred_element_type=jnp.float32
        ).reshape(sequence_length, -1)
        gated_out = (gate_sig * attended_rows).astype(jnp.bfloat16)
        grad_gated = jnp.dot(cot_rows, out_weight.T, preferred_element_type=jnp.float32)
        grad_gate = grad_gated * attended_rows * gate_sig * (1.0 - gate_sig)
        attended_gradient = (
            (grad_gated * gate_sig)
            .astype(jnp.bfloat16)
            .reshape(sequence_length, local_heads, head_size)
        )
        probability_gradient = jnp.einsum(
            "fuc,suc->ufs", attended_gradient, value_rows, preferred_element_type=jnp.float32
        )
        value_gradient = jnp.einsum(
            "avj,vat->jat", attention_probs, attended_gradient, preferred_element_type=jnp.float32
        )
        grad_score = attention * (
            probability_gradient - jnp.sum(attention * probability_gradient, -1, keepdims=True)
        )
        score_gradient = grad_score.astype(jnp.bfloat16)
        query_gradient = (
            jnp.einsum(
                "vkq,qvy->kvy", score_gradient, key_matrix, preferred_element_type=jnp.float32
            )
            * inverse_square_root
        )
        key_gradient = (
            jnp.einsum(
                "avj,vat->jat", score_gradient, query_rows, preferred_element_type=jnp.float32
            )
            * inverse_square_root
        )
        grads = jnp.stack(
            [
                query_gradient.reshape(sequence_length, -1),
                key_gradient.reshape(sequence_length, -1),
                value_gradient.reshape(sequence_length, -1),
                grad_gate,
            ]
        ).astype(jnp.bfloat16)
        weight_sums = weight_sums + jnp.einsum(
            "nd,gne->gde", hidden, grads, preferred_element_type=jnp.float32
        )
        output_sums = output_sums + jnp.dot(
            gated_out.T, cot_rows, preferred_element_type=jnp.float32
        )
        return ((bias_sums + grad_score, weight_sums, output_sums), (gated_out, grads))

    start_sums = (
        jnp.zeros((local_heads, token_count, token_count), jnp.float32),
        jnp.zeros(attn_weight.shape, jnp.float32),
        jnp.zeros(out_weight.shape, jnp.float32),
    )
    final_sums, stacked = lax.scan(one_copy, start_sums, (tokens, cotangent, scales))
    bias_sums, weight_sums, output_sums = final_sums
    gated_all, grads_all = stacked
    token_share = token_count // lax.axis_size(COL)
    attn_parts = jnp.einsum(
        "tnd,de->tne", gated_all, out_weight, preferred_element_type=jnp.float32
    )
    hidden_parts = jnp.einsum(
        "tgne,gde->tnd", grads_all, attn_weight, preferred_element_type=jnp.float32
    )
    attn_out, grad_hidden = tuple(
        (
            part.astype(jnp.float32)
            for part in side_by_side(
                (attn_parts.astype(jnp.bfloat16), hidden_parts.astype(jnp.bfloat16)), COL, 1, 0
            )
        )
    )
    first_token = col_index * token_share
    token_mine = lax.dynamic_slice_in_dim(tokens, first_token, token_share, 1)
    cot_mine = lax.dynamic_slice_in_dim(cotangent, first_token, token_share, 1)
    scaled_mine = scales[:, None, None] * token_mine.astype(jnp.float32)
    denoised = (scaled_mine + attn_out).astype(jnp.bfloat16)
    grad_scaled = cot_mine.astype(jnp.float32) + norm_back(grad_hidden, scaled_mine, attn_gain)
    token_grad = (scales[:, None, None] * grad_scaled).astype(jnp.bfloat16)
    bias_rows_sum, out_grad, weight_grad = (
        summed_on_arrival(bias_sums.astype(jnp.bfloat16), GROUP_ROW, 1),
        summed_on_arrival(output_sums.astype(jnp.bfloat16), GROUP_ROW, 1),
        summed_on_arrival(weight_sums.astype(jnp.bfloat16), GROUP_ROW, 1),
    )
    bias_back = lax.all_to_all(bias_rows_sum, COL, split_axis=2, concat_axis=0, tiled=True)
    grad_bias = jnp.transpose(bias_back, (1, 2, 0)).reshape(-1, heads_all)
    grad_in = jnp.dot(
        grad_bias, bias_weight.astype(jnp.float32).T, precision=lax.Precision.HIGHEST
    ).reshape(rows_here, cols_here, channels)
    pair_grad = norm_back(grad_in, updated, bias_gain)
    weight_part = jnp.dot(
        flat_bias.astype(jnp.float32).T, grad_bias, precision=lax.Precision.HIGHEST
    )
    bias_weight_grad = by_axis(weight_part, GROUP_ROW_COL)
    return (
        updated.astype(jnp.bfloat16),
        pair_grad,
        bias_weight_grad,
        denoised,
        token_grad,
        weight_grad,
        out_grad,
    )


def solution(mesh):
    finer = Mesh(
        mesh.devices.reshape(mesh.shape["group"], 4, 2, 4, 4),
        ("group", "row_0", "row_1", "col_0", "col_1"),
    )
    return jax.shard_map(
        shards,
        mesh=finer,
        in_specs=(
            P(GROUP_ROW, COL, None),
            P(GROUP_ROW, COL),
            P(),
            P(),
            P(),
            P(),
            P(),
            P(),
            P(),
            P(),
            P(),
            P(GROUP_ROW, None, None),
            P(GROUP_ROW),
            P(),
            P(None, None, COL),
            P(COL, None),
            P(GROUP_ROW, None, None),
        ),
        out_specs=(
            P(GROUP_ROW, COL, None),
            P(GROUP_ROW, COL, None),
            P(),
            P(GROUP_ROW, COL, None),
            P(GROUP_ROW, COL, None),
            P(None, GROUP_ROW, COL),
            P(COL, GROUP_ROW),
        ),
        check_vma=False,
    )
```

profile of v0, /device:TPU:1, one launch (start us, length us, event | category | flops | bytes accessed | tf_op | source)
XLA Modules:
  0.0 234.4 jit_solution(619105595789823685)
XLA Ops:
  13.4 7.3 %all-to-all-start = ((bf16[16,128,16,16]{1,3,2,0:T(8,128)(2,1)}), bf16[16,128,16,16]{1,3,2,0:T(8,128)(2,1)S(1)}, u32[]{:S(2)}, u32[]{:S(2)}) async-start(bf16[16,128,16,16]{1,3,2,0:T(8,128)(2,1)} %broadcast_in_dim.16), calls=%async_computation | async-start | bytes 2097152 | tf_op jit(solution)/shard_map/all_to_all | solution.py:29
  21.2 15.2 %all-to-all-done = bf16[16,128,16,16]{1,3,2,0:T(8,128)(2,1)S(1)} async-done(((bf16[16,128,16,16]{1,3,2,0:T(8,128)(2,1)}), bf16[16,128,16,16]{1,3,2,0:T(8,128)(2,1)S(1)}, u32[]{:S(2)}, u32[]{:S(2)}) %all-to-all-start) | async-done | bytes 1048608 | tf_op jit(solution)/shard_map/all_to_all | solution.py:29
  38.1 2.4 %copy.127 = bf16[128,256,16]{0,2,1:T(8,128)(2,1)} copy(bf16[128,256,16]{1,2,0:T(8,128)(2,1)S(1)} %convolution_convert_fusion.2) | data formatting | bytes 2097152 | tf_op jit(solution)/shard_map/convert_element_type | solution.py:138
  40.5 10.0 %all-to-all-start.1 = ((bf16[16,128,16,16]{1,3,2,0:T(8,128)(2,1)}), bf16[16,128,16,16]{1,3,2,0:T(8,128)(2,1)S(1)}, u32[]{:S(2)}, u32[]{:S(2)}) async-start(bf16[16,128,16,16]{1,3,2,0:T(8,128)(2,1)} %bitcast.15), calls=%async_computation.1 | async-start | bytes 2097152 | tf_op jit(solution)/shard_map/all_to_all | solution.py:44
  50.9 27.2 %all-to-all-done.1 = bf16[16,128,16,16]{1,3,2,0:T(8,128)(2,1)S(1)} async-done(((bf16[16,128,16,16]{1,3,2,0:T(8,128)(2,1)}), bf16[16,128,16,16]{1,3,2,0:T(8,128)(2,1)S(1)}, u32[]{:S(2)}, u32[]{:S(2)}) %all-to-all-start.1) | async-done | bytes 1048608 | tf_op jit(solution)/shard_map/all_to_all | solution.py:44
  80.0 14.9 %all_to_all.66 = bf16[16,2,128]{2,1,0:T(2,128)(2,1)S(1)} all-to-all(bf16[16,2,128]{2,1,0:T(2,128)(2,1)S(1)} %reshape.407), channel_id=1, replica_groups=mesh['group'=2,'row_0'=4,'row_1'=2,'col_0'=4,'col_1'=4] {'col_0','col_1'}, dimensions={0} | all-to-all | bytes 16384 | tf_op jit(solution)/shard_map/all_to_all | solution.py:155
  95.9 5.8 %all-to-all-start.3 = ((bf16[16,1,16,256]{3,2,1,0:T(8,128)(2,1)}), bf16[16,1,16,256]{3,2,1,0:T(8,128)(2,1)S(1)}, u32[]{:S(2)}, u32[]{:S(2)}) async-start(bf16[16,1,16,256]{3,2,1,0:T(8,128)(2,1)} %broadcast_in_dim.22), calls=%async_computation.3 | async-start | bytes 262144 | tf_op jit(solution)/shard_map/all_to_all | solution.py:29
  101.8 6.0 %all-to-all-done.3 = bf16[16,1,16,256]{3,2,1,0:T(8,128)(2,1)S(1)} async-done(((bf16[16,1,16,256]{3,2,1,0:T(8,128)(2,1)}), bf16[16,1,16,256]{3,2,1,0:T(8,128)(2,1)S(1)}, u32[]{:S(2)}, u32[]{:S(2)}) %all-to-all-start.3) | async-done | bytes 131104 | tf_op jit(solution)/shard_map/all_to_all | solution.py:29
  107.9 28.1 %while.19 = (s32[]{:T(128)}, f32[1,256,256]{1,2,0:T(8,128)S(1)}, f32[4,768,48]{1,2,0:T(8,128)}, f32[48,768]{1,0:T(8,128)S(1)}, bf16[3,256,48]{1,2,0:T(8,128)(2,1...) while((s32[]{:T(128)}, f32[1,256,256]{1,2,0:T(8,128)S(1)}, ...), condition=%wide.region_12.13_spmd.clone, body=%wide.region_7.12_spmd.clone.sunk | while | flops 232935168 | bytes 9195741 | solution.py:241
  110.2 2.0 fusion.133
  114.7 1.8 fusion.140
  118.9 2.0 fusion.133
  123.4 2.9 %fusion.140 = f32[4,768,48]{1,2,0:T(8,128)} fusion(f32[4,768,48]{1,2,0:T(8,128)} %get-tuple-element.383, pred[]{:T(512)S(6)} %compare.3, bf16[1,256,48]{1,2,0:T(8,128)(2,1)S(1)} %bitcast.379, bf16[1,256,48]{1,2,0:T(8,128)(2,1)S(1)} %bitcast.381, bf16[1,256,48]{1,2,0:T(8,128)(2,1)S(1)} %bitcast.374, bf16[1,256,48]{1,2,0:T(8,128)(2,1)S(1)} %bitcast.372, ...), kind=kOutput, calls=%fused_computation.1.clone.1 | convolution fusion | flops 77119488 | bytes 1677321 | tf_op jit(solution)/shard_map/while/body/eval_jaxpr/nd,gne->gde/dot_general | solution.py:228
  128.6 2.0 fusion.133
  133.1 2.9 %fusion.140 = f32[4,768,48]{1,2,0:T(8,128)} fusion(f32[4,768,48]{1,2,0:T(8,128)} %get-tuple-element.383, pred[]{:T(512)S(6)} %compare.3, bf16[1,256,48]{1,2,0:T(8,128)(2,1)S(1)} %bitcast.379, bf16[1,256,48]{1,2,0:T(8,128)(2,1)S(1)} %bitcast.381, bf16[1,256,48]{1,2,0:T(8,128)(2,1)S(1)} %bitcast.374, bf16[1,256,48]{1,2,0:T(8,128)(2,1)S(1)} %bitcast.372, ...), kind=kOutput, calls=%fused_computation.1.clone.1 | convolution fusion | flops 77119488 | bytes 1677321 | tf_op jit(solution)/shard_map/while/body/eval_jaxpr/nd,gne->gde/dot_general | solution.py:228
  136.0 1.6 bitcast_convert_fusion
  138.1 1.6 pad_maximum_fusion
  141.1 3.9 %all-to-all-start.7 = ((bf16[16,2,1152]{2,1,0:T(2,128)(2,1)}), bf16[16,2,1152]{2,1,0:T(2,128)(2,1)S(1)}, u32[]{:S(2)}, u32[]{:S(2)}) async-start(bf16[16,2,1152]{2,1,0:T(2,128)(2,1)} %reshape.413), calls=%async_computation.8 | async-start | bytes 147456 | tf_op jit(solution)/shard_map/all_to_all | solution.py:44
  145.8 5.1 %all-to-all-done.7 = bf16[16,2,1152]{2,1,0:T(2,128)(2,1)S(1)} async-done(((bf16[16,2,1152]{2,1,0:T(2,128)(2,1)}), bf16[16,2,1152]{2,1,0:T(2,128)(2,1)S(1)}, u32[]{:S(2)}, u32[]{:S(2)}) %all-to-all-start.7) | async-done | bytes 73760 | tf_op jit(solution)/shard_map/all_to_all | solution.py:44
  151.0 3.8 %all-to-all-start.4 = ((bf16[16,1,16,256]{3,2,1,0:T(8,128)(2,1)}), bf16[16,1,16,256]{3,2,1,0:T(8,128)(2,1)S(1)}, u32[]{:S(2)}, u32[]{:S(2)}) async-start(bf16[16,1,16,256]{3,2,1,0:T(8,128)(2,1)} %bitcast.25), calls=%async_computation.4 | async-start | bytes 262144 | tf_op jit(solution)/shard_map/all_to_all | solution.py:44
  154.9 1.8 convert_element_type.186
  156.7 1.9 reshape.379
  159.7 3.0 %reshape.411 = bf16[16,2,4608]{2,1,0:T(2,128)(2,1)} reshape(bf16[16,4,48,48]{3,2,1,0:T(8,128)(2,1)} %bitcast.370) | data formatting | bytes 589824
  165.3 3.7 %all-to-all-start.5 = ((f32[16,1,256]{2,1,0:T(1,128)}), f32[16,1,256]{2,1,0:T(1,128)S(1)}, u32[]{:S(2)}, u32[]{:S(2)}) async-start(f32[16,1,256]{2,1,0:T(1,128)} %reshape.409), calls=%async_computation.5 | async-start | bytes 32768 | tf_op jit(solution)/shard_map/all_to_all | solution.py:271
  169.6 8.3 %all-to-all-done.5 = f32[16,1,256]{2,1,0:T(1,128)S(1)} async-done(((f32[16,1,256]{2,1,0:T(1,128)}), f32[16,1,256]{2,1,0:T(1,128)S(1)}, u32[]{:S(2)}, u32[]{:S(2)}) %all-to-all-start.5) | async-done | bytes 16416 | tf_op jit(solution)/shard_map/all_to_all | solution.py:271
  177.9 7.1 %all-to-all-start.6 = ((bf16[16,2,4608]{2,1,0:T(2,128)(2,1)}), bf16[16,2,4608]{2,1,0:T(2,128)(2,1)S(1)}, u32[]{:S(2)}, u32[]{:S(2)}) async-start(bf16[16,2,4608]{2,1,0:T(2,128)(2,1)} %reshape.411), calls=%async_computation.7 | async-start | bytes 589824 | tf_op jit(solution)/shard_map/all_to_all | solution.py:44
  186.9 4.6 %psum.35 = f32[128,16]{0,1:T(8,128)S(1)} all-reduce(f32[128,16]{0,1:T(8,128)S(1)} %convolution_bitcast_fusion.2), channel_id=1, replica_groups=mesh['group'=2,'row_0'=4,'row_1'=2,'col_0'=4,'col_1'=4] {'group'}, use_global_device_ids=true, to_apply=%region_16.17 | all-reduce | flops 2048 | bytes 16384 | tf_op jit(solution)/shard_map/psum | solution.py:58
  191.5 8.8 %psum.36 = f32[128,16]{0,1:T(8,128)S(1)} all-reduce(f32[128,16]{0,1:T(8,128)S(1)} %psum.35), channel_id=1, replica_groups=mesh['group'=2,'row_0'=4,'row_1'=2,'col_0'=4,'col_1'=4] {'row_0'}, use_global_device_ids=true, to_apply=%region_17.18 | all-reduce | flops 2048 | bytes 16384 | tf_op jit(solution)/shard_map/psum | solution.py:58
  200.3 4.8 %psum.37 = f32[128,16]{0,1:T(8,128)S(1)} all-reduce(f32[128,16]{0,1:T(8,128)S(1)} %psum.36), channel_id=1, replica_groups=mesh['group'=2,'row_0'=4,'row_1'=2,'col_0'=4,'col_1'=4] {'row_1'}, use_global_device_ids=true, to_apply=%region_18.19 | all-reduce | flops 2048 | bytes 16384 | tf_op jit(solution)/shard_map/psum | solution.py:58
  205.1 8.7 %psum.38 = f32[128,16]{0,1:T(8,128)S(1)} all-reduce(f32[128,16]{0,1:T(8,128)S(1)} %psum.37), channel_id=1, replica_groups=mesh['group'=2,'row_0'=4,'row_1'=2,'col_0'=4,'col_1'=4] {'col_0'}, use_global_device_ids=true, to_apply=%region_19.20 | all-reduce | flops 2048 | bytes 16384 | tf_op jit(solution)/shard_map/psum | solution.py:58
  213.8 8.4 %psum.39 = f32[128,16]{0,1:T(8,128)} all-reduce(f32[128,16]{0,1:T(8,128)S(1)} %psum.38), channel_id=1, replica_groups=mesh['group'=2,'row_0'=4,'row_1'=2,'col_0'=4,'col_1'=4] {'col_1'}, use_global_device_ids=true, to_apply=%region_20.21 | all-reduce | flops 2048 | bytes 16384 | tf_op jit(solution)/shard_map/psum | solution.py:58
  225.8 1.7 multiply_convert_fusion.3
  (157 shorter events, 38.3 us)
Async XLA Ops:
  7.2 71.9 %copy-start = (bf16[128,128]{1,0:T(8,128)(2,1)S(1)}, bf16[128,128]{1,0:T(8,128)(2,1)}, u32[]{:S(2)}) copy-start(bf16[128,128]{1,0:T(8,128)(2,1)} %param.26) | copy-start | bytes 98308
  13.4 23.0 %all-to-all-start = ((bf16[16,128,16,16]{1,3,2,0:T(8,128)(2,1)}), bf16[16,128,16,16]{1,3,2,0:T(8,128)(2,1)S(1)}, u32[]{:S(2)}, u32[]{:S(2)}) async-start(bf16[16,128,16,16]{1,3,2,0:T(8,128)(2,1)} %broadcast_in_dim.16), calls=%async_computation | async-start | bytes 2097152 | tf_op jit(solution)/shard_map/all_to_all | solution.py:29
  40.5 10.0 %copy-start.7 = (s32[256]{0:T(256)S(1)}, s32[256]{0:T(256)}, u32[]{:S(2)}) copy-start(s32[256]{0:T(256)} %param.21) | copy-start | bytes 3076
  40.5 10.2 %copy-start.10 = (bf16[128,128]{1,0:T(8,128)(2,1)S(1)}, bf16[128,128]{1,0:T(8,128)(2,1)}, u32[]{:S(2)}) copy-start(bf16[128,128]{1,0:T(8,128)(2,1)} %param.24) | copy-start | bytes 98308
  40.5 37.6 %all-to-all-start.1 = ((bf16[16,128,16,16]{1,3,2,0:T(8,128)(2,1)}), bf16[16,128,16,16]{1,3,2,0:T(8,128)(2,1)S(1)}, u32[]{:S(2)}, u32[]{:S(2)}) async-start(bf16[16,128,16,16]{1,3,2,0:T(8,128)(2,1)} %bitcast.15), calls=%async_computation.1 | async-start | bytes 2097152 | tf_op jit(solution)/shard_map/all_to_all | solution.py:44
  50.5 28.4 %copy-start.8 = (f32[128]{0:T(128)S(1)}, f32[128]{0:T(128)}, u32[]{:S(2)}) copy-start(f32[128]{0:T(128)} %param.25) | copy-start | bytes 1540
  50.7 28.4 %copy-start.3 = (bf16[16,16,128]{2,1,0:T(8,128)(2,1)S(1)}, bf16[16,16,128]{2,1,0:T(8,128)(2,1)}, u32[]{:S(2)}) copy-start(bf16[16,16,128]{2,1,0:T(8,128)(2,1)} %param.19) | copy-start | bytes 196612
  50.8 28.7 %copy-start.6 = (bf16[128,16]{0,1:T(8,128)(2,1)S(1)}, bf16[128,16]{0,1:T(8,128)(2,1)}, u32[]{:S(2)}) copy-start(bf16[128,16]{0,1:T(8,128)(2,1)} %param.28) | copy-start | bytes 12292
  50.9 28.7 %copy-start.9 = (f32[128]{0:T(128)S(1)}, f32[128]{0:T(128)}, u32[]{:S(2)}) copy-start(f32[128]{0:T(128)} %param.27) | copy-start | bytes 1540
  50.9 28.7 %copy-start.11 = (f32[16]{0:T(128)S(1)}, f32[16]{0:T(128)}, u32[]{:S(2)}) copy-start(f32[16]{0:T(128)} %param.29) | copy-start | bytes 196
  78.3 23.4 %copy-start.12 = (s32[3]{0:T(128)S(1)}, s32[3]{0:T(128)}, u32[]{:S(2)}) copy-start(s32[3]{0:T(128)} %param.31) | copy-start | bytes 40
  78.8 29.1 %copy-start.2 = (bf16[3,256,768]{2,1,0:T(8,128)(2,1)S(1)}, bf16[3,256,768]{2,1,0:T(8,128)(2,1)}, u32[]{:S(2)}) copy-start(bf16[3,256,768]{2,1,0:T(8,128)(2,1)} %param.35) | copy-start | bytes 3538948
  79.0 28.9 %copy-start.1 = (bf16[3,256,768]{2,1,0:T(8,128)(2,1)S(1)}, bf16[3,256,768]{2,1,0:T(8,128)(2,1)}, u32[]{:S(2)}) copy-start(bf16[3,256,768]{2,1,0:T(8,128)(2,1)} %param.30) | copy-start | bytes 3538948
  79.0 28.9 %copy-start.4 = (bf16[48,768]{1,0:T(8,128)(2,1)S(1)}, bf16[48,768]{1,0:T(8,128)(2,1)}, u32[]{:S(2)}) copy-start(bf16[48,768]{1,0:T(8,128)(2,1)} %param.34) | copy-start | bytes 221188
  79.0 28.9 %copy-start.5 = (f32[768]{0:T(1024)S(1)}, f32[768]{0:T(1024)}, u32[]{:S(2)}) copy-start(f32[768]{0:T(1024)} %param.32) | copy-start | bytes 9220
  95.9 11.9 %all-to-all-start.3 = ((bf16[16,1,16,256]{3,2,1,0:T(8,128)(2,1)}), bf16[16,1,16,256]{3,2,1,0:T(8,128)(2,1)S(1)}, u32[]{:S(2)}, u32[]{:S(2)}) async-start(bf16[16,1,16,256]{3,2,1,0:T(8,128)(2,1)} %broadcast_in_dim.22), calls=%async_computation.3 | async-start | bytes 262144 | tf_op jit(solution)/shard_map/all_to_all | solution.py:29
  101.7 123.1 %reduce-scatter.2.cloned.1.call-start = ((), (), s32[]{:S(2)}) async-start(), calls=%async_computation.9 | async-start | bytes 2506752 | tf_op jit(solution)/shard_map/reduce_scatter | solution.py:50
  141.1 9.8 %all-to-all-start.7 = ((bf16[16,2,1152]{2,1,0:T(2,128)(2,1)}), bf16[16,2,1152]{2,1,0:T(2,128)(2,1)S(1)}, u32[]{:S(2)}, u32[]{:S(2)}) async-start(bf16[16,2,1152]{2,1,0:T(2,128)(2,1)} %reshape.413), calls=%async_computation.8 | async-start | bytes 147456 | tf_op jit(solution)/shard_map/all_to_all | solution.py:44
  151.0 11.9 %all-to-all-start.4 = ((bf16[16,1,16,256]{3,2,1,0:T(8,128)(2,1)}), bf16[16,1,16,256]{3,2,1,0:T(8,128)(2,1)S(1)}, u32[]{:S(2)}, u32[]{:S(2)}) async-start(bf16[16,1,16,256]{3,2,1,0:T(8,128)(2,1)} %bitcast.25), calls=%async_computation.4 | async-start | bytes 262144 | tf_op jit(solution)/shard_map/all_to_all | solution.py:44
  165.3 12.7 %all-to-all-start.5 = ((f32[16,1,256]{2,1,0:T(1,128)}), f32[16,1,256]{2,1,0:T(1,128)S(1)}, u32[]{:S(2)}, u32[]{:S(2)}) async-start(f32[16,1,256]{2,1,0:T(1,128)} %reshape.409), calls=%async_computation.5 | async-start | bytes 32768 | tf_op jit(solution)/shard_map/all_to_all | solution.py:271
  177.9 45.2 %all-to-all-start.6 = ((bf16[16,2,4608]{2,1,0:T(2,128)(2,1)}), bf16[16,2,4608]{2,1,0:T(2,128)(2,1)S(1)}, u32[]{:S(2)}, u32[]{:S(2)}) async-start(bf16[16,2,4608]{2,1,0:T(2,128)(2,1)} %reshape.411), calls=%async_computation.7 | async-start | bytes 589824 | tf_op jit(solution)/shard_map/all_to_all | solution.py:44
Sparse Core Ops, SparseCore 0:
  139.9 81.3 reduce-scatter.1
where the time goes:
time: 237 us; the launch traced here: 234 us
  waiting for transfers between devices  61.9 us (26%)
  blocking collectives  50.3 us (21%)
  starting transfers between devices  41.7 us (18%)
  matrix products  22.6 us (10%)
  other arithmetic  22.1 us (9%)
  local copies, waits for them, and re-layouts  21.1 us (9%)
  between operations  14.6 us (6%)
    psum x5, blocking collectives, by_axis(): return functools.reduce(lax.psum, axes, array)  35.3 us
    all_to_all x4, waiting for transfers between devices, summed_on_arrival(): lax.all_to_all(parts, axis, split_axis=0, concat_axis=0, tiled=True)  32.3 us
    all_to_all x4, starting transfers between devices, summed_on_arrival(): lax.all_to_all(parts, axis, split_axis=0, concat_axis=0, tiled=True)  24.8 us
    all_to_all x2, waiting for transfers between devices, sent_to_all(): return lax.all_to_all(copies, axis, split_axis=0, concat_axis=0, tiled=True)  21.2 us
    all_to_all x1, blocking collectives, shards(): lax.all_to_all(bias_major, COL, split_axis=0, concat_axis=2, tiled=True)  14.9 us
    all_to_all x2, starting transfers between devices, sent_to_all(): return lax.all_to_all(copies, axis, split_axis=0, concat_axis=0, tiled=True)  13.1 us
    all_to_all x1, waiting for transfers between devices, shards(): lax.all_to_all(bias_rows_sum, COL, split_axis=2, concat_axis=0, tiled=True)  8.3 us
    dot_general x3, matrix products, one_copy(): jnp.einsum('nd,gne->gde', hidden, grads, preferred_element_type=jnp.float32)  7.65 us
  transfers between devices with their start and end apart: 8, of which 5 were waited for; matrix products, arithmetic and copies ran while one was open for 8% of the time, Pallas kernels for 0%

commit v1 on v0

v1 whole, which is shorter than its diff:
```python
import math

import jax
import jax.numpy as jnp
from jax import lax
from jax.experimental import pallas as pl
from jax.experimental.pallas import tpu as pltpu
from jax.sharding import PartitionSpec as P

MESH = pl.DeviceIdType.MESH
LEVELS = 200
EPSILON = 1e-05
SIGMA_LOW = 0.1
SIGMA_SPAN = 100.0
F32 = jnp.float32
BF16 = jnp.bfloat16
S = 16
C = 128
E = 48
D = 768
N = 256
T = 3
NT = (((1,), (1,)), ((), ()))
TN = (((0,), (0,)), ((), ()))


def iota(shape, dim):
    return lax.broadcasted_iota(jnp.int32, shape, dim)


def dot(a, b):
    return jnp.dot(a, b, preferred_element_type=F32)


def dot_nt(a, b):
    return lax.dot_general(a, b, NT, preferred_element_type=F32)


def dot_tn(a, b):
    return lax.dot_general(a, b, TN, preferred_element_type=F32)


def sigmoid(v):
    return 1.0 / (1.0 + jnp.exp(-v))


def centred_inverse(v):
    centred = v - jnp.mean(v, -1, keepdims=True)
    return centred, lax.rsqrt(jnp.mean(centred * centred, -1, keepdims=True) + EPSILON)


def norm_back(gradient, values, gain):
    centred, inverse = centred_inverse(values)
    normed = centred * inverse
    weighted = gradient * gain
    return inverse * (
        weighted
        - jnp.mean(weighted, -1, keepdims=True)
        - normed * jnp.mean(weighted * normed, -1, keepdims=True)
    )


def swap_blocks(x, unit):
    arr = iota(x.shape, 0) // S
    blk = iota(x.shape, 1) // unit
    for bit in (1, 2, 4, 8):
        rows = bit * S
        other = jnp.concatenate(
            [x[(k ^ 1) * rows : (k ^ 1) * rows + rows] for k in range(N // rows)], axis=0
        )
        up = pltpu.roll(other, bit * unit, 1)
        down = pltpu.roll(other, C - bit * unit, 1)
        in_arr, in_blk = (arr & bit) != 0, (blk & bit) != 0
        x = jnp.where(in_arr == in_blk, x, jnp.where(in_blk, up, down))
    return x


def kernel(
    pair, mask, chain, tri_in_gain, tri_proj, tri_gate, tri_out_gain, tri_out, bias_gain,
    bias_weight, chain_bias, tokens, level, attn_gain, attn_weight, out_weight, cot,
    pair_next, pair_grad, bias_weight_grad, denoised, token_grad, weight_grad,
    gate_scr, r_send, l_send, r_own, l_own, r_all, left_t, t_send, t_recv, row_scr, upd_scr,
    bias_in_scr, bw_pad, b_send, b_recv, b_all, w_four, ow_pad, place, w_all, hid_scr, qkv_scr,
    sig_scr, gg_scr, raw, raw_z, part, part_x, bs_send, bs_recv, bb_send, bb_recv, ws_send,
    ws_recv, ar_one, ar_all, ar_two, ar_fin,
    sem_r, sem_l, sem_ag, sem_fw, sem_t, sem_b, sem_ba, sem_w, sem_z, sem_x, sem_bs, sem_bb,
    sem_ws, sem_a1, sem_a2,
):
    group, row, col = lax.axis_index("group"), lax.axis_index("row"), lax.axis_index("col")
    mine = group * 8 + row
    core, high = row % 2, row // 2
    quad = group * 4 + high
    zed, ex = col // 4, col % 4
    pending = []

    def send(src, dst, sem, at, device):
        copy = pltpu.make_async_remote_copy(
            src_ref=src, dst_ref=dst, send_sem=sem.at[0, at], recv_sem=sem.at[1, at],
            device_id=device, device_id_type=MESH,
        )
        copy.start()
        pending.append(copy)
        return copy

    def to_col(step):
        return {"col": (col + step) % S}

    def to_line(step):
        there = (mine + step) % S
        return {"group": there // 8, "row": there % 8}

    barrier = pltpu.get_barrier_semaphore()
    for step in range(1, S):
        pl.semaphore_signal(barrier, inc=1, device_id=to_col(step), device_id_type=MESH)
        pl.semaphore_signal(barrier, inc=1, device_id=to_line(step), device_id_type=MESH)

    tile = pair[...].astype(F32).reshape(N, C)
    centred, inverse = centred_inverse(tile)
    pair_in = (centred * inverse * tri_in_gain[...]).astype(BF16)
    pick = (iota((N, S), 0) // S == iota((N, S), 1)).astype(BF16)
    spread = dot(pick, mask[...].astype(F32).astype(BF16))
    mask_col = jnp.sum(
        jnp.where(iota((N, S), 0) % S == iota((N, S), 1), spread, 0.0), -1, keepdims=True
    )
    right = dot(pair_in, tri_proj[:, 2 * C : 4 * C])
    right = sigmoid(right[:, :C]) * right[:, C:] * mask_col
    r_send[...] = swap_blocks(right, 8).astype(BF16).reshape(S, S, C)
    pl.semaphore_wait(barrier, 2 * (S - 1))
    r_copies = [
        send(r_send.at[(col + d) % S], r_own.at[col], sem_r, d, to_col(d)) for d in range(1, S)
    ]
    r_own[col] = r_send[col]
    left = dot(pair_in, tri_proj[:, : 2 * C])
    left = sigmoid(left[:, :C]) * left[:, C:] * mask_col
    l_send[...] = swap_blocks(left, 8).astype(BF16).reshape(S, S, C)
    l_copies = [
        send(l_send.at[(col + d) % S], l_own.at[col], sem_l, d, to_col(d)) for d in range(1, S)
    ]
    l_own[col] = l_send[col]
    gate_scr[...] = sigmoid(dot(pair_in, tri_gate[...]))

    w_four[...] = jnp.zeros_like(w_four)
    for g in range(4):
        w_four[:, g * C : g * C + E] = attn_weight[g]
    ow_pad[...] = jnp.zeros_like(ow_pad)
    ow_pad[:E, :] = out_weight[...]
    bw_pad[...] = jnp.zeros_like(bw_pad)
    bw_pad[:, :S] = bias_weight[...]
    place_row = iota((5 * C, N), 0)
    inner = place_row % C
    place[...] = jnp.where(
        (inner < E) & (iota((5 * C, N), 1) == place_row // C * E + inner), 1.0, 0.0
    ).astype(BF16)

    scale_of = []
    for t in range(T):
        power = jnp.full((1, C), level[t].astype(F32)) * (math.log(SIGMA_SPAN) / (LEVELS - 1))
        sigma = SIGMA_LOW * jnp.exp(power)
        scale_of.append(lax.rsqrt(1.0 + sigma * sigma)[:, :1])
    inverse_root = 1.0 / math.sqrt(E)

    def before_bias(t):
        scaled = tokens[t].astype(F32) * scale_of[t]
        mid, inv = centred_inverse(scaled)
        hidden = (mid * inv * attn_gain[...]).astype(BF16)
        hid_scr[t] = hidden
        projections = dot(hidden, w_four[...])
        for g in range(3):
            qkv_scr[t, g] = projections[:, g * C : (g + 1) * C].astype(BF16)
        sig_scr[t] = sigmoid(projections[:, 3 * C :])
        gg_scr[t] = dot_nt(cot[t], ow_pad[...])

    before_bias(0)

    for copy in r_copies:
        copy.wait_recv()
    ag = {
        k: send(
            r_own, r_all.at[mine], sem_ag, k,
            {"group": (quad + k) % 8 // 4, "row": (quad + k) % 4 * 2 + core},
        )
        for k in range(1, 8)
    }
    partner = {"row": high * 2 + 1 - core}
    fw = {0: send(r_own, r_all.at[mine], sem_fw, 0, partner)}
    before_bias(1)
    for copy in l_copies:
        copy.wait_recv()
    left_t[...] = l_own[...].reshape(N, C).astype(F32).T.astype(BF16)
    diagonal = iota((C, C), 0) % 8 == iota((C, C), 1) % 8

    def triangle(at, block):
        product = dot(left_t[...], block.reshape(N, C))
        product = jnp.where(diagonal, product, 0.0).reshape(S, 8, C)
        t_send[at] = jnp.sum(product, axis=1).astype(BF16)

    def from_quad(k, side):
        there = (quad + 8 - k) % 8
        return there // 4 * 8 + there % 4 * 2 + side

    triangle(mine, r_own[...])
    fw[0].wait_recv()
    triangle(from_quad(0, 1 - core), r_all[from_quad(0, 1 - core)])
    before_bias(2)
    for k in range(1, 8):
        ag[k].wait_recv()
        at = from_quad(k, core)
        fw[k] = send(r_all.at[at], r_all.at[at], sem_fw, k, partner)
        triangle(at, r_all[at])
    for k in range(1, 8):
        fw[k].wait_recv()
        at = from_quad(k, 1 - core)
        triangle(at, r_all[at])
    t_copies = [
        send(t_send.at[(col + d) % S], t_recv.at[col], sem_t, d, to_col(d)) for d in range(1, S)
    ]
    t_recv[col] = t_send[col]

    packed = dot(w_four[...], place[: 4 * C, :]) + dot_tn(ow_pad[...], place[4 * C :, :])
    w_all[zed] = packed.astype(BF16)

    for copy in t_copies:
        copy.wait_recv()
    moved = swap_blocks(t_recv[...].astype(F32).reshape(N, C), 8)
    for j in range(S):
        row_scr[pl.ds(j, S, stride=S), :] = moved[j * S : (j + 1) * S]
    centred, inverse = centred_inverse(row_scr[...])
    tri_normed = (centred * inverse * tri_out_gain[...]).astype(BF16)
    tile = pair[...].astype(F32).reshape(N, C)
    updated = tile + gate_scr[...] * dot(tri_normed, tri_out[...])
    upd_scr[...] = updated
    centred, inverse = centred_inverse(updated)
    bias_in = (centred * inverse * bias_gain[...]).astype(BF16)
    bias_in_scr[...] = bias_in
    row_scr[...] = dot(bias_in, bw_pad[...])
    by_col = jnp.concatenate([row_scr[pl.ds(j, S, stride=S), :] for j in range(S)], axis=0)
    by_head = swap_blocks(by_col, 1)
    ids = chain[...].astype(F32)
    here = mine * S + iota((N, N), 0) % S
    row_chain = jnp.sum(jnp.where(iota((N, N), 1) == here, ids, 0.0), -1, keepdims=True)
    ids_col = jnp.sum(
        jnp.where(iota((N, N), 1) == iota((N, N), 0), ids, 0.0), -1, keepdims=True
    )
    there = col * S + iota((N, C), 1)
    col_chain = jnp.sum(jnp.where(iota((N, C), 0) == there, ids_col, 0.0), 0, keepdims=True)
    head_bias = jnp.sum(
        jnp.where(iota((N, S), 1) == iota((N, S), 0) // S, chain_bias[...], 0.0),
        -1, keepdims=True,
    )
    by_head = by_head + jnp.where(row_chain == col_chain, head_bias, 0.0)
    b_send[...] = by_head.astype(BF16).reshape(S, S, C)
    b_copies = [
        send(b_send.at[(col + d) % S], b_recv.at[col], sem_b, d, to_col(d)) for d in range(1, S)
    ]
    b_recv[col] = b_send[col]
    pair_next[...] = updated.astype(BF16)
    lane_block = iota((S, C), 1) // S
    for copy in b_copies:
        copy.wait_recv()
    halves = []
    for half in range(2):
        joined = jnp.zeros((S, C), F32)
        for k in range(8):
            piece = b_recv[half * 8 + k].astype(F32)
            piece = pltpu.roll(piece, k * S, 1) if k else piece
            joined = jnp.where(lane_block == k, piece, joined)
        halves.append(joined)
    b_all[mine] = jnp.concatenate(halves, axis=1).astype(BF16)
    ba_copies = [
        send(b_all.at[mine], b_all.at[mine], sem_ba, d, to_line(d)) for d in range(1, S)
    ]
    w_copies = [
        send(w_all.at[zed], w_all.at[zed], sem_w, d, {"col": (zed + d) % 4 * 4 + ex})
        for d in range(1, 4)
    ]
    for copy in ba_copies:
        copy.wait_recv()

    bias_sum = None
    z_copies, x_copies = {}, {}
    for t in range(T):
        queries, keys, values = qkv_scr[t, 0], qkv_scr[t, 1], qkv_scr[t, 2]
        gate_sig, grad_gated = sig_scr[t], gg_scr[t]
        bias = b_all[...].reshape(N, N).astype(F32)
        exponent = jnp.exp(dot_nt(queries, keys) * inverse_root + bias)
        attention = exponent / jnp.sum(exponent, -1, keepdims=True)
        attention_b = attention.astype(BF16)
        attended = dot(attention_b, values)
        gated = (gate_sig * attended).astype(BF16)
        grad_gate = (grad_gated * attended * gate_sig * (1.0 - gate_sig)).astype(BF16)
        grad_attended = (grad_gated * gate_sig).astype(BF16)
        grad_prob = dot_nt(grad_attended, values)
        grad_values = dot_tn(attention_b, grad_attended).astype(BF16)
        grad_score = attention * (
            grad_prob - jnp.sum(attention * grad_prob, -1, keepdims=True)
        )
        score_b = grad_score.astype(BF16)
        bias_sum = grad_score if bias_sum is None else bias_sum + grad_score
        grad_queries = (dot(score_b, keys) * inverse_root).astype(BF16)
        grad_keys = (dot_tn(score_b, queries) * inverse_root).astype(BF16)
        side = jnp.concatenate([grad_queries, grad_keys, grad_values, grad_gate, gated], axis=1)
        raw[t] = dot(side, place[...]).astype(BF16).reshape(4, 64, N)
        z_copies[t] = [
            send(
                raw.at[t, (zed + d) % 4], raw_z.at[t, zed], sem_z, t * 4 + d,
                {"col": (zed + d) % 4 * 4 + ex},
            )
            for d in range(1, 4)
        ]
        raw_z[t, zed] = raw[t, zed]
    bs_send[...] = bias_sum.astype(BF16).reshape(S, S, N)
    bs_copies = [
        send(bs_send.at[(mine + d) % S], bs_recv.at[mine], sem_bs, d, to_line(d))
        for d in range(1, S)
    ]
    bs_recv[mine] = bs_send[mine]

    raw_t = raw[...].reshape(T * N, N).astype(F32).T.astype(BF16)
    grads_part = dot(raw_t[: 4 * E], hid_scr[...].reshape(T * N, D))
    out_part = dot(raw_t[4 * E :], cot[...].reshape(T * N, D))
    turned = jnp.concatenate([grads_part, out_part], axis=0).T
    ws_send[...] = turned.astype(BF16).reshape(S, E, N)
    ws_copies = [
        send(ws_send.at[(mine + d) % S], ws_recv.at[mine], sem_ws, d, to_line(d))
        for d in range(1, S)
    ]
    ws_recv[mine] = ws_send[mine]
    for copy in w_copies:
        copy.wait_recv()

    def project(t):
        for copy in z_copies[t]:
            copy.wait_recv()
        total = jnp.zeros((C, D), F32)
        first = iota((64, N), 1) < 4 * E
        for z in range(4):
            piece = raw_z[t, z].astype(F32)
            both = jnp.concatenate(
                [jnp.where(first, piece, 0.0), jnp.where(first, 0.0, piece)], axis=0
            ).astype(BF16)
            total = total + dot_nt(both, w_all[z])
        total = total.astype(BF16)
        for x in range(4):
            part[t, x, 0] = total[x * S : (x + 1) * S]
            part[t, x, 1] = total[64 + x * S : 64 + (x + 1) * S]
        x_copies[t] = [
            send(
                part.at[t, (ex + d) % 4], part_x.at[t, d - 1], sem_x, t * 4 + d,
                {"col": zed * 4 + (ex + d) % 4},
            )
            for d in range(1, 4)
        ]

    def finish(t):
        for copy in x_copies[t]:
            copy.wait_recv()
        sums = part[t, ex].astype(F32)
        for d in range(3):
            sums = sums + part_x[t, d].astype(F32)
        first = pl.multiple_of(col * S, S)
        scaled = tokens[t, pl.ds(first, S), :].astype(F32) * scale_of[t]
        cot_mine = cot[t, pl.ds(first, S), :].astype(F32)
        denoised[t] = (scaled + sums[1]).astype(BF16)
        back = norm_back(sums[0], scaled, attn_gain[...])
        token_grad[t] = (scale_of[t] * (cot_mine + back)).astype(BF16)

    project(0)
    for copy in bs_copies:
        copy.wait_recv()
    bias_rows = jnp.sum(bs_recv[...].astype(F32), axis=0)
    narrow = iota((S, C), 1) < S
    for k in range(S):
        piece = bias_rows[:, :C] if k < 8 else bias_rows[:, C:]
        piece = pltpu.roll(piece, C - k % 8 * S, 1) if k % 8 else piece
        bb_send[k] = jnp.where(narrow, piece, 0.0).astype(BF16)
    bb_copies = [
        send(bb_send.at[(col + d) % S], bb_recv.at[col], sem_bb, d, to_col(d))
        for d in range(1, S)
    ]
    bb_recv[col] = bb_send[col]
    project(1)
    project(2)
    for copy in bb_copies:
        copy.wait_recv()
    back = swap_blocks(bb_recv[...].astype(F32).reshape(N, C), 1)
    back = jnp.where(iota((N, C), 1) < S, back, 0.0)
    for j in range(S):
        row_scr[pl.ds(j, S, stride=S), :] = back[j * S : (j + 1) * S]
    grad_bias = row_scr[...].astype(BF16)
    ar_one[...] = dot_tn(grad_bias, bias_in_scr[...])[:S]
    a1_copies = [
        send(ar_one, ar_all.at[mine], sem_a1, d, to_line(d)) for d in range(1, S)
    ]
    ar_all[mine] = ar_one[...]
    grad_in = dot_nt(grad_bias, bw_pad[...])
    pair_grad[...] = norm_back(grad_in, upd_scr[...], bias_gain[...])
    finish(0)
    for copy in a1_copies:
        copy.wait_recv()
    ar_two[...] = jnp.sum(ar_all[...], axis=0)
    a2_copies = [
        send(ar_two, ar_fin.at[col], sem_a2, d, to_col(d)) for d in range(1, S)
    ]
    ar_fin[col] = ar_two[...]
    finish(1)
    finish(2)
    for copy in ws_copies:
        copy.wait_recv()
    weight_grad[...] = jnp.sum(ws_recv[...].astype(F32), axis=0)
    for copy in a2_copies:
        copy.wait_recv()
    bias_weight_grad[...] = jnp.sum(ar_fin[...], axis=0)
    for copy in pending:
        copy.wait_send()


def shards(
    pair_repr, pair_mask, chain_id, tri_in_gain, tri_proj, tri_gate, tri_out_gain, tri_out,
    bias_gain, bias_weight, chain_bias, tokens, noise_level, attn_gain, attn_weight, out_weight,
    cotangent,
):
    vmem = pl.BlockSpec(memory_space=pltpu.VMEM)
    smem = pl.BlockSpec(memory_space=pltpu.SMEM)

    def buf(*shape, kind=BF16):
        return pltpu.VMEM(shape, kind)

    def sems(count):
        return pltpu.SemaphoreType.DMA((2, count))

    outs = pl.pallas_call(
        kernel,
        out_shape=(
            jax.ShapeDtypeStruct((N, C), BF16),
            jax.ShapeDtypeStruct((N, C), F32),
            jax.ShapeDtypeStruct((S, C), F32),
            jax.ShapeDtypeStruct((T, S, D), BF16),
            jax.ShapeDtypeStruct((T, S, D), BF16),
            jax.ShapeDtypeStruct((E, N), F32),
        ),
        in_specs=[vmem] * 12 + [smem] + [vmem] * 4,
        out_specs=(vmem,) * 6,
        scratch_shapes=[
            buf(N, C, kind=F32),
            buf(S, S, C), buf(S, S, C), buf(S, S, C), buf(S, S, C),
            buf(S, S, S, C),
            buf(C, N),
            buf(S, S, C), buf(S, S, C),
            buf(N, C, kind=F32), buf(N, C, kind=F32),
            buf(N, C), buf(C, C),
            buf(S, S, C), buf(S, S, C), buf(S, S, N),
            buf(D, 4 * C), buf(C, D), buf(5 * C, N), buf(4, D, N),
            buf(T, N, D), buf(T, 3, N, C),
            buf(T, N, C, kind=F32), buf(T, N, C, kind=F32),
            buf(T, 4, 64, N), buf(T, 4, 64, N),
            buf(T, 4, 2, S, D), buf(T, 3, 2, S, D),
            buf(S, S, N), buf(S, S, N), buf(S, S, C), buf(S, S, C),
            buf(S, E, N), buf(S, E, N),
            buf(S, C, kind=F32), buf(S, S, C, kind=F32),
            buf(S, C, kind=F32), buf(S, S, C, kind=F32),
            sems(S), sems(S), sems(8), sems(8), sems(S), sems(S), sems(S), sems(4),
            sems(12), sems(12), sems(S), sems(S), sems(S), sems(S), sems(S),
        ],
        compiler_params=pltpu.CompilerParams(
            collective_id=0, has_side_effects=True, vmem_limit_bytes=60 * 1024 * 1024
        ),
    )(
        pair_repr, pair_mask, chain_id.reshape(1, N), tri_in_gain.reshape(1, C), tri_proj,
        tri_gate, tri_out_gain.reshape(1, C), tri_out, bias_gain.reshape(1, C), bias_weight,
        chain_bias.reshape(1, S), tokens, noise_level, attn_gain.reshape(1, D), attn_weight,
        out_weight, cotangent,
    )
    pair_next, pair_grad, bias_weight_grad, denoised, token_grad, weight_grad = outs
    grads = weight_grad[:, : 4 * E].reshape(E, 4, E)
    return (
        pair_next.reshape(S, S, C),
        pair_grad.reshape(S, S, C),
        bias_weight_grad.T,
        denoised,
        token_grad,
        jnp.transpose(grads, (1, 0, 2)),
        weight_grad[:, 4 * E : 5 * E].T,
    )


def solution(mesh):
    line, col = ("group", "row"), "col"
    return jax.shard_map(
        shards,
        mesh=mesh,
        in_specs=(
            P(line, col, None), P(line, col), P(), P(), P(), P(), P(), P(), P(), P(), P(),
            P(line, None, None), P(line), P(), P(None, None, col), P(col, None),
            P(line, None, None),
        ),
        out_specs=(
            P(line, col, None), P(line, col, None), P(), P(line, col, None),
            P(line, col, None), P(None, line, col), P(col, line),
        ),
        check_vma=False,
    )
```

time: 237 us -> 127 us (0.54)
  Pallas kernels: 0 us -> 110 us
  waiting for transfers between devices: 61.9 us -> 0 us
  blocking collectives: 50.3 us -> 0 us
  starting transfers between devices: 41.7 us -> 0 us
  matrix products: 22.6 us -> 0 us
  other arithmetic: 22.1 us -> 0 us
  between operations: 14.6 us -> 0.65 us
  local copies, waits for them, and re-layouts: 21.1 us -> 15.2 us
    pallas_call x0 -> x1, Pallas kernels: none -> 110 us  [shards(): pl.pallas_call(kernel, out_shape=(jax.ShapeDtypeStruct((N, C), BF16), jax...]
    all_to_all x7 -> x0, waiting for transfers between devices: 61.8 us -> none  [the longest x4 32.3 us: summed_on_arrival(): lax.all_to_all(parts, axis, split_axis=0, concat_axis=0, tiled=True)]
    all_to_all x7 -> x0, starting transfers between devices: 41.6 us -> none  [the longest x4 24.8 us: summed_on_arrival(): lax.all_to_all(parts, axis, split_axis=0, concat_axis=0, tiled=True)]
    psum x5 -> x0, blocking collectives: 35.3 us -> none  [by_axis(): return functools.reduce(lax.psum, axes, array)]
    dot_general x36 -> x0, matrix products: 16.7 us -> none  [the longest x3 7.65 us: one_copy(): jnp.einsum('nd,gne->gde', hidden, grads, preferred_element_type=jnp.float32)]
    all_to_all x1 -> x0, blocking collectives: 14.9 us -> none  [shards(): lax.all_to_all(bias_major, COL, split_axis=0, concat_axis=2, tiled=True)]
    reduce_sum x18 -> x0, other arithmetic: 9.84 us -> none  [the longest x5 3.82 us: normalize(): jnp.mean(centred * centred, -1, keepdims=True) + EPSILON]
    while x3 -> x0, matrix products: 5.96 us -> none
  transfers between devices with their start and end apart: 8 -> 0, of which waited for: 5 -> 0; matrix products, arithmetic and copies ran while one was open for 8% -> 0% of each run, Pallas kernels for 0% -> 0%
where the time goes in v1:
time: 127 us; the launch traced here: 126 us
  Pallas kernels  110 us (87%)
  local copies, waits for them, and re-layouts  15.2 us (12%)
    pallas_call x1, Pallas kernels, shards(): pl.pallas_call(kernel, out_shape=(jax.ShapeDtypeStruct((N, C), BF16), jax...  110 us
    unnamed x8, local copies, waits for them, and re-layouts  11.6 us

profile of v1, /device:TPU:1, one launch (start us, length us, event | category | flops | bytes accessed | tf_op | source)
XLA Modules:
  0.0 126.1 jit_solution(12592351969517451893)
XLA Ops:
  0.6 1.3 %reshape.46.attn_gain = f32[1,768]{1,0:T(1,128)} reshape(f32[768]{0:T(1024)} %param.30) | data formatting | bytes 6144 | tf_op jit(solution)/shard_map/reshape | solution.py:470
  1.9 1.4 %copy.24.bias_weight = bf16[128,16]{1,0:T(8,128)(2,1)} copy(bf16[128,16]{0,1:T(8,128)(2,1)} %param.26) | data formatting | bytes 8192 | tf_op args[9]
  3.3 2.1 %copy.25.attn_weight = bf16[4,768,48]{2,1,0:T(8,128)(2,1)} copy(bf16[4,768,48]{1,2,0:T(8,128)(2,1)} %param.31) | data formatting | bytes 589824 | tf_op args[14]
  5.4 110.3 %shard_map.216 = (bf16[256,128]{1,0:T(8,128)(2,1)}, f32[256,128]{1,0:T(8,128)}, f32[16,128]{1,0:T(8,128)}, bf16[3,16,768]{2,1,0:T(8,128)(2,1)}, bf16[3,16,768]{2,1,0:T(8,128)(2,1)}, /*index=5*/f32[48,256]{1,0:T(8,128)}) custom-call(bf16[16,16,128]{2,1,0:T(8,128)(2,1)} %pair.1, s32[16,16]{1,0:T(8,128)} %mask.1, s32[1,256]{1,0:T(1,128)} %bitcast.19, ...), custom_call_target="tpu_custom_call" | custom-call | tf_op jit(solution)/shard_map/pallas_call | solution.py:431
  115.7 0.8 slice_bitcast_fusion
  116.5 0.7 copy.27
  117.2 0.9 reshape.49
  118.1 0.6 copy.29
  118.7 1.5 %copy.35 = bf16[16,16,128]{2,1,0:T(8,128)(2,1)} copy(bf16[16,16,128]{2,1,0:T(8,128)(2,1)} %bitcast.17) | data formatting | bytes 131072
  120.2 1.6 %copy.36 = f32[16,16,128]{2,1,0:T(8,128)} copy(f32[16,16,128]{2,1,0:T(8,128)} %bitcast.14) | data formatting | bytes 262144
  121.8 1.3 %copy.37 = f32[128,16]{0,1:T(8,128)} copy(f32[128,16]{0,1:T(8,128)} %bitcast.18) | data formatting | bytes 16384
  123.1 1.5 %copy.38 = bf16[3,16,768]{2,1,0:T(8,128)(2,1)} copy(bf16[3,16,768]{2,1,0:T(8,128)(2,1)} %get-tuple-element.36) | data formatting | bytes 147456
  124.6 1.5 %copy.39 = bf16[3,16,768]{2,1,0:T(8,128)(2,1)} copy(bf16[3,16,768]{2,1,0:T(8,128)(2,1)} %get-tuple-element.37) | data formatting | bytes 147456

commit v2 on v1

--- a/solution.py
+++ b/solution.py
@@ -80,11 +80,11 @@
     bias_weight, chain_bias, tokens, level, attn_gain, attn_weight, out_weight, cot,
     pair_next, pair_grad, bias_weight_grad, denoised, token_grad, weight_grad,
     gate_scr, r_send, l_send, r_own, l_own, r_all, left_t, t_send, t_recv, row_scr, upd_scr,
-    bias_in_scr, bw_pad, b_send, b_recv, b_all, w_four, ow_pad, place, w_all, hid_scr, qkv_scr,
+    bias_in_scr, bw_pad, b_send, b_recv, b_all, w_four, ow_pad, place, w_own, w_rem, hid_scr, qkv_scr,
     sig_scr, gg_scr, raw, raw_z, part, part_x, bs_send, bs_recv, bb_send, bb_recv, ws_send,
     ws_recv, ar_one, ar_all, ar_two, ar_fin,
-    sem_r, sem_l, sem_ag, sem_fw, sem_t, sem_b, sem_ba, sem_w, sem_z, sem_x, sem_bs, sem_bb,
-    sem_ws, sem_a1, sem_a2,
+    sem_r, sem_l, sem_ag, sem_fw, sem_t, sem_b, sem_ba, sem_w, sem_wg, sem_wf, sem_z, sem_x,
+    sem_bs, sem_bb, sem_ws, sem_a1, sem_a2,
 ):
     group, row, col = lax.axis_index("group"), lax.axis_index("row"), lax.axis_index("col")
     mine = group * 8 + row
@@ -139,13 +139,21 @@
     l_own[col] = l_send[col]
     gate_scr[...] = sigmoid(dot(pair_in, tri_gate[...]))
 
+    for g in range(4):
+        w_own[3 * g : 3 * g + 3] = attn_weight[g].reshape(3, S, D)
+    w_own[12:15] = out_weight[...].reshape(3, S, D)
+    w_own[15] = jnp.zeros((S, D), BF16)
+    w_copies = [
+        send(w_own.at[mine], w_rem.at[mine, d - 1], sem_w, d, {"col": (zed + 4 - d) % 4 * 4 + ex})
+        for d in range(1, 4)
+    ]
     w_four[...] = jnp.zeros_like(w_four)
     for g in range(4):
-        w_four[:, g * C : g * C + E] = attn_weight[g]
+        w_four[g * C : g * C + E, :] = attn_weight[g]
     ow_pad[...] = jnp.zeros_like(ow_pad)
     ow_pad[:E, :] = out_weight[...]
     bw_pad[...] = jnp.zeros_like(bw_pad)
-    bw_pad[:, :S] = bias_weight[...]
+    bw_pad[:S, :] = bias_weight[...]
     place_row = iota((5 * C, N), 0)
     inner = place_row % C
     place[...] = jnp.where(
@@ -162,9 +170,9 @@
     def before_bias(t):
         scaled = tokens[t].astype(F32) * scale_of[t]
         mid, inv = centred_inverse(scaled)
-        hidden = (mid * inv * attn_gain[...]).astype(BF16)
+        hidden = (mid * inv * attn_gain[...].reshape(1, D)).astype(BF16)
         hid_scr[t] = hidden
-        projections = dot(hidden, w_four[...])
+        projections = dot_nt(hidden, w_four[...])
         for g in range(3):
             qkv_scr[t, g] = projections[:, g * C : (g + 1) * C].astype(BF16)
         sig_scr[t] = sigmoid(projections[:, 3 * C :])
@@ -216,8 +224,16 @@
     ]
     t_recv[col] = t_send[col]
 
-    packed = dot(w_four[...], place[: 4 * C, :]) + dot_tn(ow_pad[...], place[4 * C :, :])
-    w_all[zed] = packed.astype(BF16)
+    for copy in w_copies:
+        copy.wait_recv()
+    wg = [
+        send(
+            w_rem.at[mine], w_rem.at[mine], sem_wg, k,
+            {"group": (quad + k) % 8 // 4, "row": (quad + k) % 4 * 2 + core},
+        )
+        for k in range(1, 8)
+    ]
+    wf = [send(w_rem.at[mine], w_rem.at[mine], sem_wf, 0, partner)]
 
     for copy in t_copies:
         copy.wait_recv()
@@ -232,7 +248,7 @@
     centred, inverse = centred_inverse(updated)
     bias_in = (centred * inverse * bias_gain[...]).astype(BF16)
     bias_in_scr[...] = bias_in
-    row_scr[...] = dot(bias_in, bw_pad[...])
+    row_scr[...] = dot_nt(bias_in, bw_pad[...])
     by_col = jnp.concatenate([row_scr[pl.ds(j, S, stride=S), :] for j in range(S)], axis=0)
     by_head = swap_blocks(by_col, 1)
     ids = chain[...].astype(F32)
@@ -269,10 +285,10 @@
     ba_copies = [
         send(b_all.at[mine], b_all.at[mine], sem_ba, d, to_line(d)) for d in range(1, S)
     ]
-    w_copies = [
-        send(w_all.at[zed], w_all.at[zed], sem_w, d, {"col": (zed + d) % 4 * 4 + ex})
-        for d in range(1, 4)
-    ]
+    for k in range(1, 8):
+        wg[k - 1].wait_recv()
+        at = from_quad(k, core)
+        wf.append(send(w_rem.at[at], w_rem.at[at], sem_wf, k, partner))
     for copy in ba_copies:
         copy.wait_recv()
 
@@ -300,20 +316,20 @@
         grad_keys = (dot_tn(score_b, queries) * inverse_root).astype(BF16)
         side = jnp.concatenate([grad_queries, grad_keys, grad_values, grad_gate, gated], axis=1)
         raw[t] = dot(side, place[...]).astype(BF16).reshape(4, 64, N)
+        if t == T - 1:
+            bs_send[...] = bias_sum.astype(BF16).reshape(S, S, N)
+            bs_copies = [
+                send(bs_send.at[(mine + d) % S], bs_recv.at[mine], sem_bs, d, to_line(d))
+                for d in range(1, S)
+            ]
+            bs_recv[mine] = bs_send[mine]
         z_copies[t] = [
             send(
-                raw.at[t, (zed + d) % 4], raw_z.at[t, zed], sem_z, t * 4 + d,
-                {"col": (zed + d) % 4 * 4 + ex},
+                raw.at[t, (zed + 4 - d) % 4], raw_z.at[t, d - 1], sem_z, t * 4 + d,
+                {"col": (zed + 4 - d) % 4 * 4 + ex},
             )
             for d in range(1, 4)
         ]
-        raw_z[t, zed] = raw[t, zed]
-    bs_send[...] = bias_sum.astype(BF16).reshape(S, S, N)
-    bs_copies = [
-        send(bs_send.at[(mine + d) % S], bs_recv.at[mine], sem_bs, d, to_line(d))
-        for d in range(1, S)
-    ]
-    bs_recv[mine] = bs_send[mine]
 
     raw_t = raw[...].reshape(T * N, N).astype(F32).T.astype(BF16)
     grads_part = dot(raw_t[: 4 * E], hid_scr[...].reshape(T * N, D))
@@ -325,7 +341,7 @@
         for d in range(1, S)
     ]
     ws_recv[mine] = ws_send[mine]
-    for copy in w_copies:
+    for copy in wf:
         copy.wait_recv()
 
     def project(t):
@@ -333,12 +349,13 @@
             copy.wait_recv()
         total = jnp.zeros((C, D), F32)
         first = iota((64, N), 1) < 4 * E
-        for z in range(4):
-            piece = raw_z[t, z].astype(F32)
+        for d in range(4):
+            piece = (raw_z[t, d - 1] if d else raw[t, zed]).astype(F32)
+            weights = w_rem[:, d - 1] if d else w_own[...]
             both = jnp.concatenate(
                 [jnp.where(first, piece, 0.0), jnp.where(first, 0.0, piece)], axis=0
             ).astype(BF16)
-            total = total + dot_nt(both, w_all[z])
+            total = total + dot(both, weights.reshape(N, D))
         total = total.astype(BF16)
         for x in range(4):
             part[t, x, 0] = total[x * S : (x + 1) * S]
@@ -361,7 +378,7 @@
         scaled = tokens[t, pl.ds(first, S), :].astype(F32) * scale_of[t]
         cot_mine = cot[t, pl.ds(first, S), :].astype(F32)
         denoised[t] = (scaled + sums[1]).astype(BF16)
-        back = norm_back(sums[0], scaled, attn_gain[...])
+        back = norm_back(sums[0], scaled, attn_gain[...].reshape(1, D))
         token_grad[t] = (scale_of[t] * (cot_mine + back)).astype(BF16)
 
     project(0)
@@ -392,7 +409,7 @@
         send(ar_one, ar_all.at[mine], sem_a1, d, to_line(d)) for d in range(1, S)
     ]
     ar_all[mine] = ar_one[...]
-    grad_in = dot_nt(grad_bias, bw_pad[...])
+    grad_in = dot(grad_bias, bw_pad[...])
     pair_grad[...] = norm_back(grad_in, upd_scr[...], bias_gain[...])
     finish(0)
     for copy in a1_copies:
@@ -412,6 +429,15 @@
     bias_weight_grad[...] = jnp.sum(ar_fin[...], axis=0)
     for copy in pending:
         copy.wait_send()
+
+
+def finisher(*refs):
+    sums = refs[5]
+    for at in range(5):
+        refs[6 + at][...] = refs[at][...]
+    for g in range(4):
+        refs[11][g] = sums[:, g * E : (g + 1) * E]
+    refs[12][...] = pltpu.roll(sums[:, C:], C // 2, 1).T[:E]
 
 
 def shards(
@@ -449,37 +475,51 @@
             buf(N, C, kind=F32), buf(N, C, kind=F32),
             buf(N, C), buf(C, C),
             buf(S, S, C), buf(S, S, C), buf(S, S, N),
-            buf(D, 4 * C), buf(C, D), buf(5 * C, N), buf(4, D, N),
+            buf(4 * C, D), buf(C, D), buf(5 * C, N),
+            buf(S, S, D), buf(S, 3, S, D),
             buf(T, N, D), buf(T, 3, N, C),
             buf(T, N, C, kind=F32), buf(T, N, C, kind=F32),
-            buf(T, 4, 64, N), buf(T, 4, 64, N),
+            buf(T, 4, 64, N), buf(T, 3, 64, N),
             buf(T, 4, 2, S, D), buf(T, 3, 2, S, D),
             buf(S, S, N), buf(S, S, N), buf(S, S, C), buf(S, S, C),
             buf(S, E, N), buf(S, E, N),
             buf(S, C, kind=F32), buf(S, S, C, kind=F32),
             buf(S, C, kind=F32), buf(S, S, C, kind=F32),
-            sems(S), sems(S), sems(8), sems(8), sems(S), sems(S), sems(S), sems(4),
-            sems(12), sems(12), sems(S), sems(S), sems(S), sems(S), sems(S),
+            sems(S), sems(S), sems(8), sems(8), sems(S), sems(S), sems(S), sems(4), sems(8),
+            sems(8), sems(12), sems(12), sems(S), sems(S), sems(S), sems(S), sems(S),
         ],
         compiler_params=pltpu.CompilerParams(
             collective_id=0, has_side_effects=True, vmem_limit_bytes=60 * 1024 * 1024
         ),
     )(
         pair_repr, pair_mask, chain_id.reshape(1, N), tri_in_gain.reshape(1, C), tri_proj,
-        tri_gate, tri_out_gain.reshape(1, C), tri_out, bias_gain.reshape(1, C), bias_weight,
-        chain_bias.reshape(1, S), tokens, noise_level, attn_gain.reshape(1, D), attn_weight,
-        out_weight, cotangent,
-    )
-    pair_next, pair_grad, bias_weight_grad, denoised, token_grad, weight_grad = outs
-    grads = weight_grad[:, : 4 * E].reshape(E, 4, E)
+        tri_gate, tri_out_gain.reshape(1, C), tri_out, bias_gain.reshape(1, C), bias_weight.T,
+        chain_bias.reshape(1, S), tokens, noise_level, attn_gain,
+        jnp.transpose(attn_weight, (0, 2, 1)), out_weight, cotangent,
+    )
+    outs = pl.pallas_call(
+        finisher,
+        out_shape=(
+            jax.ShapeDtypeStruct((N, C), BF16),
+            jax.ShapeDtypeStruct((N, C), F32),
+            jax.ShapeDtypeStruct((S, C), F32),
+            jax.ShapeDtypeStruct((T, S, D), BF16),
+            jax.ShapeDtypeStruct((T, S, D), BF16),
+            jax.ShapeDtypeStruct((4, E, E), F32),
+            jax.ShapeDtypeStruct((E, E), F32),
+        ),
+        in_specs=[vmem] * 6,
+        out_specs=(vmem,) * 7,
+    )(*outs)
+    pair_next, pair_grad, bias_weight_grad, denoised, token_grad, weight_grad, out_grad = outs
     return (
         pair_next.reshape(S, S, C),
         pair_grad.reshape(S, S, C),
         bias_weight_grad.T,
         denoised,
         token_grad,
-        jnp.transpose(grads, (1, 0, 2)),
-        weight_grad[:, 4 * E : 5 * E].T,
+        weight_grad,
+        out_grad,
     )
 
 

time: 127 us -> 86.4 us (0.68)
  Pallas kernels: 110 us -> 85.6 us
  local copies, waits for them, and re-layouts: 15.2 us -> 0 us
    pallas_call x1, Pallas kernels: 110 us -> 83.8 us  [shards(): pl.pallas_call(kernel, out_shape=(jax.ShapeDtypeStruct((N, C), BF16), jax...]
    unnamed x8 -> x0, local copies, waits for them, and re-layouts: 11.6 us -> none
    reshape x3 -> x0, local copies, waits for them, and re-layouts: 2.82 us -> none  [the longest x2 1.55 us: shards(): grads = weight_grad[:, :4 * E].reshape(E, 4, E)]
    pallas_call x0 -> x1, Pallas kernels: none -> 1.84 us  [shards(): pl.pallas_call(finisher, out_shape=(jax.ShapeDtypeStruct((N, C), BF16), j...]
where the time goes in v2:
time: 86.4 us; the launch traced here: 86.3 us
  Pallas kernels  85.6 us (99%)
    pallas_call x1, Pallas kernels, shards(): pl.pallas_call(kernel, out_shape=(jax.ShapeDtypeStruct((N, C), BF16), jax...  83.8 us
    pallas_call x1, Pallas kernels, shards(): pl.pallas_call(finisher, out_shape=(jax.ShapeDtypeStruct((N, C), BF16), j...  1.84 us

profile of v2, /device:TPU:1, one launch (start us, length us, event | category | flops | bytes accessed | tf_op | source)
XLA Modules:
  0.0 86.3 jit_solution(7820126616929830019)
XLA Ops:
  0.6 83.8 %shard_map.216 = (bf16[256,128]{1,0:T(8,128)(2,1)}, f32[256,128]{1,0:T(8,128)}, f32[16,128]{1,0:T(8,128)}, bf16[3,16,768]{2,1,0:T(8,128)(2,1)}, bf16[3,16,768]{2,1,0:T(8,128)(2,1)}, /*index=5*/f32[48,256]{1,0:T(8,128)}) custom-call(bf16[16,16,128]{2,1,0:T(8,128)(2,1)} %pair.1, s32[16,16]{1,0:T(8,128)} %mask.1, s32[1,256]{1,0:T(1,128)} %bitcast.12, ...), custom_call_target="tpu_custom_call" | custom-call | tf_op jit(solution)/shard_map/pallas_call | solution.py:457
  84.4 1.8 %shard_map.217 = (bf16[256,128]{1,0:T(8,128)(2,1)}, f32[256,128]{1,0:T(8,128)}, f32[16,128]{1,0:T(8,128)}, bf16[3,16,768]{2,1,0:T(8,128)(2,1)}, bf16[3,16,768]{2...) custom-call(bf16[256,128]{1,0:T(8,128)(2,1)} %get-tuple-element.20.refs_0_, ...), custom_call_target="tpu_custom_call" | custom-call | tf_op jit(solution)/shard_map/pallas_call | solution.py:500

commit v3 on v2

v3 whole, which is shorter than its diff:
```python
import math

import jax
import jax.numpy as jnp
from jax import lax
from jax.experimental import pallas as pl
from jax.experimental.pallas import tpu as pltpu
from jax.sharding import PartitionSpec as P

MESH = pl.DeviceIdType.MESH
LEVELS = 200
EPSILON = 1e-05
SIGMA_LOW = 0.1
SIGMA_SPAN = 100.0
F32 = jnp.float32
BF16 = jnp.bfloat16
S = 16
C = 128
E = 48
D = 768
N = 256
T = 3
NT = (((1,), (1,)), ((), ()))
TN = (((0,), (0,)), ((), ()))


def iota(shape, dim):
    return lax.broadcasted_iota(jnp.int32, shape, dim)


def dot(a, b):
    return jnp.dot(a, b, preferred_element_type=F32)


def dot_nt(a, b):
    return lax.dot_general(a, b, NT, preferred_element_type=F32)


def dot_tn(a, b):
    return lax.dot_general(a, b, TN, preferred_element_type=F32)


def sigmoid(v):
    return 1.0 / (1.0 + jnp.exp(-v))


def centred_inverse(v):
    centred = v - jnp.mean(v, -1, keepdims=True)
    return centred, lax.rsqrt(jnp.mean(centred * centred, -1, keepdims=True) + EPSILON)


def norm_back(gradient, values, gain):
    centred, inverse = centred_inverse(values)
    normed = centred * inverse
    weighted = gradient * gain
    return inverse * (
        weighted
        - jnp.mean(weighted, -1, keepdims=True)
        - normed * jnp.mean(weighted * normed, -1, keepdims=True)
    )


def swap_blocks(x, unit):
    arr = iota(x.shape, 0) // S
    blk = iota(x.shape, 1) // unit
    for bit in (1, 2, 4, 8):
        rows = bit * S
        other = jnp.concatenate(
            [x[(k ^ 1) * rows : (k ^ 1) * rows + rows] for k in range(N // rows)], axis=0
        )
        up = pltpu.roll(other, bit * unit, 1)
        down = pltpu.roll(other, C - bit * unit, 1)
        in_arr, in_blk = (arr & bit) != 0, (blk & bit) != 0
        x = jnp.where(in_arr == in_blk, x, jnp.where(in_blk, up, down))
    return x


def swap_rows(x):
    arr, blk = iota(x.shape, 0), iota(x.shape, 1) // S
    for bit in (1, 2, 4, 8):
        in_arr, in_blk = (arr & bit) != 0, (blk & bit) != 0
        other = jnp.where(in_arr, pltpu.roll(x, bit, 0), pltpu.roll(x, S - bit, 0))
        up = pltpu.roll(other, bit * S, 1)
        down = pltpu.roll(other, N - bit * S, 1)
        x = jnp.where(in_arr == in_blk, x, jnp.where(in_blk, up, down))
    return x


def kernel(
    *refs,
):
    (
        pair, mask, chain, tri_in_gain, tri_proj, tri_gate, tri_out_gain, tri_out, bias_gain,
        bias_weight, chain_bias, tokens, level, attn_gain, attn_weight, out_weight, cot,
    ) = refs[23:40]
    results, sem_out = refs[-7:-1], refs[-1]
    pair_next, pair_grad, bias_weight_grad, denoised, token_grad, weight_grad = results
    work(
        refs[:17], refs[23:40], refs[40], refs[17:23], results, sem_out,
        pair, mask, chain, tri_in_gain, tri_proj, tri_gate, tri_out_gain, tri_out, bias_gain,
        bias_weight, chain_bias, tokens, level, attn_gain, attn_weight, out_weight, cot,
        pair_next, pair_grad, bias_weight_grad, denoised, token_grad, weight_grad, *refs[41:-7],
    )


def work(
    stored, loaded, sem_in, given, results, sem_out,
    pair, mask, chain, tri_in_gain, tri_proj, tri_gate, tri_out_gain, tri_out, bias_gain,
    bias_weight, chain_bias, tokens, level, attn_gain, attn_weight, out_weight, cot,
    pair_next, pair_grad, bias_weight_grad, denoised, token_grad, weight_grad,
    gate_scr, r_send, l_send, r_own, l_own, r_all, left_t, t_send, t_recv, row_scr, upd_scr,
    bias_in_scr, bw_pad, b_send, b_recv, b_all, w_four, ow_pad, place, w_own, w_rem, hid_scr, qkv_scr,
    sig_scr, slope_scr, ga_scr, score_scr, prob_scr, raw, raw_z, part, part_x, bs_send, bs_recv, bb_send, bb_recv, ws_send,
    ws_recv, ar_one, ar_all, ar_two, ar_fin,
    sems,
):
    group, row, col = lax.axis_index("group"), lax.axis_index("row"), lax.axis_index("col")
    mine = group * 8 + row
    core, high = row % 2, row // 2
    quad = group * 4 + high
    zed, ex = col // 4, col % 4
    keys, bulks = {}, {}

    def send(src, dst, key, device):
        at = keys.setdefault(key, len(keys))
        pltpu.make_async_remote_copy(
            src_ref=src, dst_ref=dst, send_sem=sems.at[0, at], recv_sem=sems.at[1, at],
            device_id=device, device_id_type=MESH,
        ).start()

    def arrive(key, bulk):
        bulks[key] = bulk
        pltpu.make_async_copy(bulk, bulk, sems.at[1, keys[key]]).wait()

    def col_at(step):
        return (zed + step // 4) % 4 * 4 + (ex + step % 4) % 4

    def to_col(step):
        return {"col": col_at(step)}

    def to_line(step):
        there = (mine + step) % S
        return {"group": there // 8, "row": there % 8}

    stores = [
        pltpu.make_async_copy(src, dst, sem_out.at[k])
        for k, (src, dst) in enumerate(zip(results, given, strict=True))
    ]
    barrier = pltpu.get_barrier_semaphore()
    for step in range(1, S):
        pl.semaphore_signal(barrier, inc=1, device_id=to_col(step), device_id_type=MESH)
        pl.semaphore_signal(barrier, inc=1, device_id=to_line(step), device_id_type=MESH)

    loads = [
        pltpu.make_async_copy(src, dst, sem_in.at[k])
        for k, (src, dst) in enumerate(zip(stored, loaded, strict=True))
    ]
    first, second = (0, 1, 3, 4, 5), (14, 15, 9, 11, 12, 13, 16, 2, 6, 7, 8, 10)
    for k in first + second:
        loads[k].start()
    for k in first:
        loads[k].wait()
    tile = pair[...].astype(F32).reshape(N, C)
    centred, inverse = centred_inverse(tile)
    pair_in = (centred * inverse * tri_in_gain[...]).astype(BF16)
    pick = (iota((N, S), 0) // S == iota((N, S), 1)).astype(BF16)
    spread = dot(pick, mask[...].astype(F32).astype(BF16))
    mask_col = jnp.sum(
        jnp.where(iota((N, S), 0) % S == iota((N, S), 1), spread, 0.0), -1, keepdims=True
    )
    right = dot(pair_in, tri_proj[:, 2 * C : 4 * C])
    right = sigmoid(right[:, :C]) * right[:, C:] * mask_col
    r_send[...] = swap_blocks(right, 8).astype(BF16).reshape(S, S, C)
    pl.semaphore_wait(barrier, 2 * (S - 1))
    for d in range(1, S):
        send(r_send.at[col_at(d)], r_own.at[col], ("r", d // 4), to_col(d))
    r_own[col] = r_send[col]
    left = dot(pair_in, tri_proj[:, : 2 * C])
    left = sigmoid(left[:, :C]) * left[:, C:] * mask_col
    l_send[...] = swap_blocks(left, 8).astype(BF16).reshape(S, S, C)
    for d in range(1, S):
        send(l_send.at[col_at(d)], l_own.at[col], "l", to_col(d))
    l_own[col] = l_send[col]
    gate_scr[...] = sigmoid(dot(pair_in, tri_gate[...]))

    for k in second:
        loads[k].wait()
    for g in range(4):
        w_own[3 * g : 3 * g + 3] = attn_weight[g].reshape(3, S, D)
    w_own[12:15] = out_weight[...].reshape(3, S, D)
    w_own[15] = jnp.zeros((S, D), BF16)
    w_four[...] = jnp.zeros_like(w_four)
    for g in range(4):
        w_four[g * C : g * C + E, :] = attn_weight[g]
    ow_pad[...] = jnp.zeros_like(ow_pad)
    ow_pad[:E, :] = out_weight[...]
    bw_pad[...] = jnp.zeros_like(bw_pad)
    bw_pad[:S, :] = bias_weight[...]
    place_row = iota((5 * C, N), 0)
    inner = place_row % C
    place[...] = jnp.where(
        (inner < E) & (iota((5 * C, N), 1) == place_row // C * E + inner), 1.0, 0.0
    ).astype(BF16)

    scale_of = []
    for t in range(T):
        power = jnp.full((1, C), level[t].astype(F32)) * (math.log(SIGMA_SPAN) / (LEVELS - 1))
        sigma = SIGMA_LOW * jnp.exp(power)
        scale_of.append(lax.rsqrt(1.0 + sigma * sigma)[:, :1])
    inverse_root = 1.0 / math.sqrt(E)

    def before_bias(t):
        scaled = tokens[t].astype(F32) * scale_of[t]
        mid, inv = centred_inverse(scaled)
        hidden = (mid * inv * attn_gain[...].reshape(1, D)).astype(BF16)
        hid_scr[t] = hidden
        projections = dot_nt(hidden, w_four[...])
        for g in range(3):
            qkv_scr[t, g] = projections[:, g * C : (g + 1) * C].astype(BF16)
        gate_sig = sigmoid(projections[:, 3 * C :])
        grad_gated = dot_nt(cot[t], ow_pad[...])
        grad_attended = (grad_gated * gate_sig).astype(BF16)
        sig_scr[t] = gate_sig
        slope_scr[t] = grad_gated * gate_sig * (1.0 - gate_sig)
        ga_scr[t] = grad_attended
        score_scr[t] = dot_nt(qkv_scr[t, 0], qkv_scr[t, 1]) * inverse_root
        prob_scr[t] = dot_nt(grad_attended, qkv_scr[t, 2])

    before_bias(0)

    partner = {"row": high * 2 + 1 - core}

    def to_quad(k):
        return {"group": (quad + k) % 8 // 4, "row": (quad + k) % 4 * 2 + core}

    def from_quad(k, side):
        there = (quad + 8 - k) % 8
        return there // 4 * 8 + there % 4 * 2 + side

    def z_block(dz):
        return pl.ds((zed + 4 - dz) % 4 * 4, 4)

    def ag_key(dz, k):
        return ("ag", dz, k) if dz == 2 else ("ag", dz)

    def fw_key(dz, k):
        return ("fw", dz, k) if dz == 2 else ("fw", dz)

    def spread_right(dz):
        arrive(("r", dz), r_own.at[pl.ds(0, 4 if dz else 3)])
        block = r_own.at[z_block(dz)]
        there = r_all.at[mine, z_block(dz)]
        for k in range(1, 8):
            send(block, there, ag_key(dz, k), to_quad(k))
        send(block, there, fw_key(dz, 0), partner)

    def relay(dz, k):
        block = r_all.at[from_quad(k, core), z_block(dz)]
        send(block, block, fw_key(dz, k), partner)

    spread_right(0)
    spread_right(1)
    spread_right(3)
    spread_right(2)
    before_bias(1)
    arrive("l", l_own.at[pl.ds(0, S - 1)])
    for d in range(1, 4):
        send(w_own.at[mine], w_rem.at[mine, d - 1], "w", {"col": (zed + 4 - d) % 4 * 4 + ex})
    left_t[...] = l_own[...].reshape(N, C).astype(F32).T.astype(BF16)
    diagonal = iota((C, C), 0) % 8 == iota((C, C), 1) % 8

    def triangle(at, block):
        product = dot(left_t[...], block.reshape(N, C))
        product = jnp.where(diagonal, product, 0.0).reshape(S, 8, C)
        t_send[at] = jnp.sum(product, axis=1).astype(BF16)

    triangle(mine, r_own[...])
    for dz in (0, 1, 3):
        arrive(("ag", dz), r_all.at[pl.ds(0, 7), pl.ds(0, 4)])
        for k in range(1, 8):
            relay(dz, k)
    before_bias(2)
    for k in range(1, 8):
        arrive(("ag", 2, k), r_all.at[0, pl.ds(0, 4)])
        relay(2, k)
        triangle(from_quad(k, core), r_all[from_quad(k, core)])
    for dz in (0, 1, 3):
        arrive(("fw", dz), r_all.at[pl.ds(0, 8), pl.ds(0, 4)])
    for k in range(8):
        arrive(("fw", 2, k), r_all.at[0, pl.ds(0, 4)])
        triangle(from_quad(k, 1 - core), r_all[from_quad(k, 1 - core)])
    for d in range(1, S):
        send(t_send.at[col_at(d)], t_recv.at[col], "t", to_col(d))
    t_recv[col] = t_send[col]

    arrive("w", w_rem.at[0])
    for k in range(1, 8):
        send(w_rem.at[mine], w_rem.at[mine], "wg", to_quad(k))
    send(w_rem.at[mine], w_rem.at[mine], "wf", partner)

    arrive("t", t_recv.at[pl.ds(0, S - 1)])
    moved = swap_blocks(t_recv[...].astype(F32).reshape(N, C), 8)
    for j in range(S):
        row_scr[pl.ds(j, S, stride=S), :] = moved[j * S : (j + 1) * S]
    centred, inverse = centred_inverse(row_scr[...])
    tri_normed = (centred * inverse * tri_out_gain[...]).astype(BF16)
    tile = pair[...].astype(F32).reshape(N, C)
    updated = tile + gate_scr[...] * dot(tri_normed, tri_out[...])
    upd_scr[...] = updated
    centred, inverse = centred_inverse(updated)
    bias_in = (centred * inverse * bias_gain[...]).astype(BF16)
    bias_in_scr[...] = bias_in
    by_head = dot_nt(bw_pad[:S, :], bias_in)
    ids = chain[...].astype(F32)
    eye = iota((N, N), 0) == iota((N, N), 1)
    ids_col = jnp.sum(jnp.where(eye, ids, 0.0), -1, keepdims=True)
    lane = iota((N, N), 1)
    row_of = mine * S + lane // S == iota((N, N), 0)
    row_chain = jnp.sum(jnp.where(row_of, ids_col, 0.0), 0, keepdims=True)
    col_of = col * S + lane % S == iota((N, N), 0)
    col_chain = jnp.sum(jnp.where(col_of, ids_col, 0.0), 0, keepdims=True)
    head_bias = jnp.sum(
        jnp.where(iota((S, S), 1) == iota((S, S), 0), chain_bias[...], 0.0), -1, keepdims=True
    )
    by_head = by_head + jnp.where(row_chain == col_chain, head_bias, 0.0)
    for k in range(S):
        b_send[k] = by_head[k : k + 1]
    for d in range(1, S):
        send(b_send.at[col_at(d)], b_recv.at[col], "b", to_col(d))
    b_recv[col] = b_send[col]
    pair_next[...] = updated.astype(BF16)
    stores[0].start()
    arrive("b", b_recv.at[pl.ds(0, S - 1)])
    by_row = swap_rows(jnp.concatenate([b_recv[k] for k in range(S)], axis=0))
    b_all[mine] = by_row.astype(BF16)
    for d in range(1, S):
        send(b_all.at[mine], b_all.at[mine], "ba", to_line(d))
    arrive("wg", w_rem.at[pl.ds(0, 7)])
    for k in range(1, 8):
        at = from_quad(k, core)
        send(w_rem.at[at], w_rem.at[at], "wf", partner)
    arrive("ba", b_all.at[pl.ds(0, S - 1)])

    bias = b_all[...].reshape(N, N).astype(F32)
    copies = range(T)
    exponent = [jnp.exp(score_scr[t] + bias) for t in copies]
    attention = [e / jnp.sum(e, -1, keepdims=True) for e in exponent]
    attention_b = [a.astype(BF16) for a in attention]
    grad_score = [
        a * (prob_scr[t] - jnp.sum(a * prob_scr[t], -1, keepdims=True))
        for t, a in enumerate(attention)
    ]
    bs_send[...] = sum(grad_score[1:], grad_score[0]).astype(BF16).reshape(S, S, N)
    for d in range(1, S):
        send(bs_send.at[(mine + d) % S], bs_recv.at[mine], "bs", to_line(d))
    bs_recv[mine] = bs_send[mine]
    score_b = [g.astype(BF16) for g in grad_score]
    attended = [dot(attention_b[t], qkv_scr[t, 2]) for t in copies]
    grad_values = [dot_tn(attention_b[t], ga_scr[t]).astype(BF16) for t in copies]
    grad_queries = [(dot(score_b[t], qkv_scr[t, 1]) * inverse_root).astype(BF16) for t in copies]
    grad_keys = [(dot_tn(score_b[t], qkv_scr[t, 0]) * inverse_root).astype(BF16) for t in copies]
    gated = [(sig_scr[t] * attended[t]).astype(BF16) for t in copies]
    grad_gate = [(slope_scr[t] * attended[t]).astype(BF16) for t in copies]
    for t in copies:
        side = jnp.concatenate(
            [grad_queries[t], grad_keys[t], grad_values[t], grad_gate[t], gated[t]], axis=1
        )
        raw[t] = dot(side, place[...]).astype(BF16).reshape(4, 64, N)
    def spread_raw(t):
        for d in (2, 1, 3):
            there = (zed + 4 - d) % 4
            send(raw.at[t, there], raw_z.at[t, d - 1], ("z", t), {"col": there * 4 + ex})

    spread_raw(0)
    raw_t = raw[...].reshape(T * N, N).astype(F32).T.astype(BF16)
    grads_part = dot(raw_t[: 4 * E], hid_scr[...].reshape(T * N, D))
    out_part = dot(raw_t[4 * E :], cot[...].reshape(T * N, D))
    turned = jnp.concatenate([grads_part, out_part], axis=0).T
    ws_send[...] = turned.astype(BF16).reshape(S, E, N)
    for d in range(1, S):
        send(ws_send.at[(mine + d) % S], ws_recv.at[mine], "ws", to_line(d))
    ws_recv[mine] = ws_send[mine]
    def project(t):
        arrive(("z", t), raw_z.at[t])
        total = jnp.zeros((C, D), F32)
        first = iota((64, N), 1) < 4 * E
        for d in range(4):
            piece = (raw_z[t, d - 1] if d else raw[t, zed]).astype(F32)
            weights = w_rem[:, d - 1] if d else w_own[...]
            both = jnp.concatenate(
                [jnp.where(first, piece, 0.0), jnp.where(first, 0.0, piece)], axis=0
            ).astype(BF16)
            total = total + dot(both, weights.reshape(N, D))
        total = total.astype(BF16)
        for x in range(4):
            part[t, x, 0] = total[x * S : (x + 1) * S]
            part[t, x, 1] = total[64 + x * S : 64 + (x + 1) * S]
        for d in range(1, 4):
            there = (ex + d) % 4
            send(part.at[t, there], part_x.at[t, d - 1], ("x", t), {"col": zed * 4 + there})

    def finish(t):
        arrive(("x", t), part_x.at[t])
        sums = part[t, ex].astype(F32)
        for d in range(3):
            sums = sums + part_x[t, d].astype(F32)
        first = pl.multiple_of(col * S, S)
        scaled = tokens[t, pl.ds(first, S), :].astype(F32) * scale_of[t]
        cot_mine = cot[t, pl.ds(first, S), :].astype(F32)
        denoised[t] = (scaled + sums[1]).astype(BF16)
        back = norm_back(sums[0], scaled, attn_gain[...].reshape(1, D))
        token_grad[t] = (scale_of[t] * (cot_mine + back)).astype(BF16)

    arrive("bs", bs_recv.at[pl.ds(0, S - 1)])
    by_tile = swap_rows(jnp.sum(bs_recv[...].astype(F32), axis=0))
    for k in range(S):
        bb_send[k] = by_tile[k : k + 1]
    for d in range(1, S):
        send(bb_send.at[col_at(d)], bb_recv.at[col], "bb", to_col(d))
    bb_recv[col] = bb_send[col]
    arrive("wf", w_rem.at[pl.ds(0, 8)])
    project(0)
    spread_raw(1)
    spread_raw(2)
    arrive("bb", bb_recv.at[pl.ds(0, S - 1)])
    grad_bias = jnp.concatenate([bb_recv[k] for k in range(S)], axis=0).astype(BF16)
    ar_one[...] = dot(grad_bias, bias_in_scr[...]).astype(BF16)
    for d in range(1, S):
        send(ar_one, ar_all.at[mine], "a1", to_line(d))
    ar_all[mine] = ar_one[...]
    grad_in = dot_tn(grad_bias, bw_pad[:S, :])
    pair_grad[...] = norm_back(grad_in, upd_scr[...], bias_gain[...])
    stores[1].start()
    project(1)
    arrive("a1", ar_all.at[pl.ds(0, S - 1)])
    ar_two[...] = jnp.sum(ar_all[...].astype(F32), axis=0).astype(BF16)
    for d in range(1, S):
        send(ar_two, ar_fin.at[col], "a2", to_col(d))
    ar_fin[col] = ar_two[...]
    project(2)
    finish(0)
    finish(1)
    finish(2)
    stores[3].start()
    stores[4].start()
    arrive("ws", ws_recv.at[pl.ds(0, S - 1)])
    weight_grad[...] = jnp.sum(ws_recv[...].astype(F32), axis=0)
    stores[5].start()
    arrive("a2", ar_fin.at[pl.ds(0, S - 1)])
    bias_weight_grad[...] = jnp.sum(ar_fin[...].astype(F32), axis=0)
    stores[2].start()
    for key, bulk in bulks.items():
        pltpu.make_async_copy(bulk, bulk, sems.at[0, keys[key]]).wait()
    for copy in stores:
        copy.wait()


def finisher(*refs):
    sums = refs[5]
    for at in range(5):
        refs[6 + at][...] = refs[at][...]
    for g in range(4):
        refs[11][g] = sums[:, g * E : (g + 1) * E]
    refs[12][...] = pltpu.roll(sums[:, C:], C // 2, 1).T[:E]


def shards(
    pair_repr, pair_mask, chain_id, tri_in_gain, tri_proj, tri_gate, tri_out_gain, tri_out,
    bias_gain, bias_weight, chain_bias, tokens, noise_level, attn_gain, attn_weight, out_weight,
    cotangent,
):
    vmem = pl.BlockSpec(memory_space=pltpu.VMEM)
    hbm = pl.BlockSpec(memory_space=pltpu.HBM)

    def buf(*shape, kind=BF16):
        return pltpu.VMEM(shape, kind)

    outs = pl.pallas_call(
        kernel,
        out_shape=(
            jax.ShapeDtypeStruct((N, C), BF16),
            jax.ShapeDtypeStruct((N, C), F32),
            jax.ShapeDtypeStruct((S, C), F32),
            jax.ShapeDtypeStruct((T, S, D), BF16),
            jax.ShapeDtypeStruct((T, S, D), BF16),
            jax.ShapeDtypeStruct((E, N), F32),
        ),
        in_specs=[hbm] * 17,
        out_specs=(hbm,) * 6,
        scratch_shapes=[
            buf(S, S, C), buf(S, S, kind=jnp.int32), buf(1, N, kind=jnp.int32),
            buf(1, C, kind=F32), buf(C, 4 * C), buf(C, C), buf(1, C, kind=F32), buf(C, C),
            buf(1, C, kind=F32), buf(S, C), buf(1, S, kind=F32), buf(T, N, D),
            pltpu.SMEM((T,), jnp.int32), buf(D, kind=F32), buf(4, E, D), buf(E, D), buf(T, N, D),
            pltpu.SemaphoreType.DMA((17,)),
            buf(N, C, kind=F32),
            buf(S, S, C), buf(S, S, C), buf(S, S, C), buf(S, S, C),
            buf(S, S, S, C),
            buf(C, N),
            buf(S, S, C), buf(S, S, C),
            buf(N, C, kind=F32), buf(N, C, kind=F32),
            buf(N, C), buf(C, C),
            buf(S, 1, N, kind=F32), buf(S, 1, N, kind=F32), buf(S, S, N),
            buf(4 * C, D), buf(C, D), buf(5 * C, N),
            buf(S, S, D), buf(S, 3, S, D),
            buf(T, N, D), buf(T, 3, N, C),
            buf(T, N, C, kind=F32), buf(T, N, C, kind=F32), buf(T, N, C),
            buf(T, N, N, kind=F32), buf(T, N, N, kind=F32),
            buf(T, 4, 64, N), buf(T, 3, 64, N),
            buf(T, 4, 2, S, D), buf(T, 3, 2, S, D),
            buf(S, S, N), buf(S, S, N),
            buf(S, 1, N, kind=F32), buf(S, 1, N, kind=F32),
            buf(S, E, N), buf(S, E, N),
            buf(S, C), buf(S, S, C), buf(S, C), buf(S, S, C),
            pltpu.SemaphoreType.DMA((2, 44)),
            buf(N, C), buf(N, C, kind=F32), buf(S, C, kind=F32), buf(T, S, D), buf(T, S, D),
            buf(E, N, kind=F32), pltpu.SemaphoreType.DMA((6,)),
        ],
        compiler_params=pltpu.CompilerParams(
            collective_id=0, has_side_effects=True, vmem_limit_bytes=60 * 1024 * 1024
        ),
    )(
        pair_repr, pair_mask, chain_id.reshape(1, N), tri_in_gain.reshape(1, C), tri_proj,
        tri_gate, tri_out_gain.reshape(1, C), tri_out, bias_gain.reshape(1, C), bias_weight.T,
        chain_bias.reshape(1, S), tokens, noise_level, attn_gain,
        jnp.transpose(attn_weight, (0, 2, 1)), out_weight, cotangent,
    )
    outs = pl.pallas_call(
        finisher,
        out_shape=(
            jax.ShapeDtypeStruct((N, C), BF16),
            jax.ShapeDtypeStruct((N, C), F32),
            jax.ShapeDtypeStruct((S, C), F32),
            jax.ShapeDtypeStruct((T, S, D), BF16),
            jax.ShapeDtypeStruct((T, S, D), BF16),
            jax.ShapeDtypeStruct((4, E, E), F32),
            jax.ShapeDtypeStruct((E, E), F32),
        ),
        in_specs=[vmem] * 6,
        out_specs=(vmem,) * 7,
    )(*outs)
    pair_next, pair_grad, bias_weight_grad, denoised, token_grad, weight_grad, out_grad = outs
    return (
        pair_next.reshape(S, S, C),
        pair_grad.reshape(S, S, C),
        bias_weight_grad.T,
        denoised,
        token_grad,
        weight_grad,
        out_grad,
    )


def solution(mesh):
    line, col = ("group", "row"), "col"
    return jax.shard_map(
        shards,
        mesh=mesh,
        in_specs=(
            P(line, col, None), P(line, col), P(), P(), P(), P(), P(), P(), P(), P(), P(),
            P(line, None, None), P(line), P(), P(None, None, col), P(col, None),
            P(line, None, None),
        ),
        out_specs=(
            P(line, col, None), P(line, col, None), P(), P(line, col, None),
            P(line, col, None), P(None, line, col), P(col, line),
        ),
        check_vma=False,
    )
```

time: 86.4 us -> 75.1 us (0.87)
  Pallas kernels: 85.6 us -> 74.3 us
    pallas_call x1, Pallas kernels: 83.8 us -> 72.4 us  [shards(): pl.pallas_call(kernel, out_shape=(jax.ShapeDtypeStruct((N, C), BF16), jax...]
where the time goes in v3:
time: 75.1 us; the launch traced here: 74.9 us
  Pallas kernels  74.3 us (99%)
    pallas_call x1, Pallas kernels, shards(): pl.pallas_call(kernel, out_shape=(jax.ShapeDtypeStruct((N, C), BF16), jax...  72.4 us
    pallas_call x1, Pallas kernels, shards(): pl.pallas_call(finisher, out_shape=(jax.ShapeDtypeStruct((N, C), BF16), j...  1.84 us

profile of v3, /device:TPU:1, one launch (start us, length us, event | category | flops | bytes accessed | tf_op | source)
XLA Modules:
  0.0 74.9 jit_solution(12290099803761559380)
XLA Ops:
  0.6 72.4 %shard_map.216 = (bf16[256,128]{1,0:T(8,128)(2,1)}, f32[256,128]{1,0:T(8,128)}, f32[16,128]{1,0:T(8,128)}, bf16[3,16,768]{2,1,0:T(8,128)(2,1)}, bf16[3,16,768]{2,1,0:T(8,128)(2,1)}, /*index=5*/f32[48,256]{1,0:T(8,128)}) custom-call(bf16[16,16,128]{2,1,0:T(8,128)(2,1)} %refs_0_.1, s32[16,16]{1,0:T(8,128)} %refs_1_.1, s32[1,256]{1,0:T(1,128)} %bitcast.12, ...), custom_call_target="tpu_custom_call" | custom-call | tf_op jit(solution)/shard_map/pallas_call | solution.py:478
  73.1 1.8 %shard_map.217 = (bf16[256,128]{1,0:T(8,128)(2,1)}, f32[256,128]{1,0:T(8,128)}, f32[16,128]{1,0:T(8,128)}, bf16[3,16,768]{2,1,0:T(8,128)(2,1)}, bf16[3,16,768]{2...) custom-call(bf16[256,128]{1,0:T(8,128)(2,1)} %get-tuple-element.20.refs_0_, ...), custom_call_target="tpu_custom_call" | custom-call | tf_op jit(solution)/shard_map/pallas_call | solution.py:528

commit v4 on v3

--- a/solution.py
+++ b/solution.py
@@ -111,7 +111,7 @@
     gate_scr, r_send, l_send, r_own, l_own, r_all, left_t, t_send, t_recv, row_scr, upd_scr,
     bias_in_scr, bw_pad, b_send, b_recv, b_all, w_four, ow_pad, place, w_own, w_rem, hid_scr, qkv_scr,
     sig_scr, slope_scr, ga_scr, score_scr, prob_scr, raw, raw_z, part, part_x, bs_send, bs_recv, bb_send, bb_recv, ws_send,
-    ws_recv, ar_one, ar_all, ar_two, ar_fin,
+    ws_half, ws_sum, ws_recv, ar_one, ar_all, ar_two, ar_fin,
     sems,
 ):
     group, row, col = lax.axis_index("group"), lax.axis_index("row"), lax.axis_index("col")
@@ -292,11 +292,6 @@
     for d in range(1, S):
         send(t_send.at[col_at(d)], t_recv.at[col], "t", to_col(d))
     t_recv[col] = t_send[col]
-
-    arrive("w", w_rem.at[0])
-    for k in range(1, 8):
-        send(w_rem.at[mine], w_rem.at[mine], "wg", to_quad(k))
-    send(w_rem.at[mine], w_rem.at[mine], "wf", partner)
 
     arrive("t", t_recv.at[pl.ds(0, S - 1)])
     moved = swap_blocks(t_recv[...].astype(F32).reshape(N, C), 8)
@@ -327,6 +322,10 @@
         b_send[k] = by_head[k : k + 1]
     for d in range(1, S):
         send(b_send.at[col_at(d)], b_recv.at[col], "b", to_col(d))
+    arrive("w", w_rem.at[0])
+    for k in range(1, 8):
+        send(w_rem.at[mine], w_rem.at[mine], "wg", to_quad(k))
+    send(w_rem.at[mine], w_rem.at[mine], "wf", partner)
     b_recv[col] = b_send[col]
     pair_next[...] = updated.astype(BF16)
     stores[0].start()
@@ -335,10 +334,6 @@
     b_all[mine] = by_row.astype(BF16)
     for d in range(1, S):
         send(b_all.at[mine], b_all.at[mine], "ba", to_line(d))
-    arrive("wg", w_rem.at[pl.ds(0, 7)])
-    for k in range(1, 8):
-        at = from_quad(k, core)
-        send(w_rem.at[at], w_rem.at[at], "wf", partner)
     arrive("ba", b_all.at[pl.ds(0, S - 1)])
 
     bias = b_all[...].reshape(N, N).astype(F32)
@@ -376,10 +371,13 @@
     grads_part = dot(raw_t[: 4 * E], hid_scr[...].reshape(T * N, D))
     out_part = dot(raw_t[4 * E :], cot[...].reshape(T * N, D))
     turned = jnp.concatenate([grads_part, out_part], axis=0).T
-    ws_send[...] = turned.astype(BF16).reshape(S, E, N)
-    for d in range(1, S):
-        send(ws_send.at[(mine + d) % S], ws_recv.at[mine], "ws", to_line(d))
-    ws_recv[mine] = ws_send[mine]
+    for k in range(S):
+        ws_send[k % 2, k // 2] = turned[k * E : (k + 1) * E].astype(BF16)
+    send(ws_send.at[1 - core], ws_half, "wh", partner)
+    arrive("wg", w_rem.at[pl.ds(0, 7)])
+    for k in range(1, 8):
+        at = from_quad(k, core)
+        send(w_rem.at[at], w_rem.at[at], "wf", partner)
     def project(t):
         arrive(("z", t), raw_z.at[t])
         total = jnp.zeros((C, D), F32)
@@ -418,10 +416,12 @@
     for d in range(1, S):
         send(bb_send.at[col_at(d)], bb_recv.at[col], "bb", to_col(d))
     bb_recv[col] = bb_send[col]
+    spread_raw(1)
+    spread_raw(2)
+    arrive("wh", ws_half)
+    ws_sum[...] = (ws_send[core].astype(F32) + ws_half[...].astype(F32)).astype(BF16)
     arrive("wf", w_rem.at[pl.ds(0, 8)])
     project(0)
-    spread_raw(1)
-    spread_raw(2)
     arrive("bb", bb_recv.at[pl.ds(0, S - 1)])
     grad_bias = jnp.concatenate([bb_recv[k] for k in range(S)], axis=0).astype(BF16)
     ar_one[...] = dot(grad_bias, bias_in_scr[...]).astype(BF16)
@@ -431,19 +431,22 @@
     grad_in = dot_tn(grad_bias, bw_pad[:S, :])
     pair_grad[...] = norm_back(grad_in, upd_scr[...], bias_gain[...])
     stores[1].start()
+    for k in range(1, 8):
+        send(ws_sum.at[(quad + k) % 8], ws_recv.at[quad], "ws", to_quad(k))
+    ws_recv[quad] = ws_sum[quad]
     project(1)
+    project(2)
     arrive("a1", ar_all.at[pl.ds(0, S - 1)])
     ar_two[...] = jnp.sum(ar_all[...].astype(F32), axis=0).astype(BF16)
     for d in range(1, S):
         send(ar_two, ar_fin.at[col], "a2", to_col(d))
     ar_fin[col] = ar_two[...]
-    project(2)
     finish(0)
     finish(1)
     finish(2)
     stores[3].start()
     stores[4].start()
-    arrive("ws", ws_recv.at[pl.ds(0, S - 1)])
+    arrive("ws", ws_recv.at[pl.ds(0, 7)])
     weight_grad[...] = jnp.sum(ws_recv[...].astype(F32), axis=0)
     stores[5].start()
     arrive("a2", ar_fin.at[pl.ds(0, S - 1)])
@@ -510,21 +513,21 @@
             buf(T, 4, 2, S, D), buf(T, 3, 2, S, D),
             buf(S, S, N), buf(S, S, N),
             buf(S, 1, N, kind=F32), buf(S, 1, N, kind=F32),
-            buf(S, E, N), buf(S, E, N),
+            buf(2, 8, E, N), buf(8, E, N), buf(8, E, N), buf(8, E, N),
             buf(S, C), buf(S, S, C), buf(S, C), buf(S, S, C),
-            pltpu.SemaphoreType.DMA((2, 44)),
+            pltpu.SemaphoreType.DMA((2, 45)),
             buf(N, C), buf(N, C, kind=F32), buf(S, C, kind=F32), buf(T, S, D), buf(T, S, D),
             buf(E, N, kind=F32), pltpu.SemaphoreType.DMA((6,)),
         ],
         compiler_params=pltpu.CompilerParams(
-            collective_id=0, has_side_effects=True, vmem_limit_bytes=60 * 1024 * 1024
+            collective_id=0, has_side_effects=True, vmem_limit_bytes=30 * 1024 * 1024
         ),
-    )(
+    )(*[pltpu.with_memory_space_constraint(array, pltpu.HBM) for array in (
         pair_repr, pair_mask, chain_id.reshape(1, N), tri_in_gain.reshape(1, C), tri_proj,
         tri_gate, tri_out_gain.reshape(1, C), tri_out, bias_gain.reshape(1, C), bias_weight.T,
         chain_bias.reshape(1, S), tokens, noise_level, attn_gain,
         jnp.transpose(attn_weight, (0, 2, 1)), out_weight, cotangent,
-    )
+    )])
     outs = pl.pallas_call(
         finisher,
         out_shape=(
@@ -538,6 +541,7 @@
         ),
         in_specs=[vmem] * 6,
         out_specs=(vmem,) * 7,
+        compiler_params=pltpu.CompilerParams(vmem_limit_bytes=4 * 1024 * 1024),
     )(*outs)
     pair_next, pair_grad, bias_weight_grad, denoised, token_grad, weight_grad, out_grad = outs
     return (

time: 75.1 us -> 70 us (0.932)
  Pallas kernels: 74.3 us -> 69.2 us
    pallas_call x1, Pallas kernels: 72.4 us -> 68.4 us  [shards(): pl.pallas_call(kernel, out_shape=(jax.ShapeDtypeStruct((N, C), BF16), jax...]
    pallas_call x1, Pallas kernels: 1.84 us -> 0.8 us  [shards(): pl.pallas_call(finisher, out_shape=(jax.ShapeDtypeStruct((N, C), BF16), j...]
where the time goes in v4:
time: 70 us; the launch traced here: 69.9 us
  Pallas kernels  69.2 us (99%)
    pallas_call x1, Pallas kernels, shards(): pl.pallas_call(kernel, out_shape=(jax.ShapeDtypeStruct((N, C), BF16), jax...  68.4 us

profile of v4, /device:TPU:1, one launch (start us, length us, event | category | flops | bytes accessed | tf_op | source)
XLA Modules:
  0.0 69.9 jit_solution(3971166504748793170)
XLA Ops:
  0.6 68.4 %shard_map.216 = (bf16[256,128]{1,0:T(8,128)(2,1)S(1)}, f32[256,128]{1,0:T(8,128)S(1)}, f32[16,128]{1,0:T(8,128)S(1)}, bf16[3,16,768]{2,1,0:T(8,128)(2,1)S(1)}, ...) custom-call(bf16[16,16,128]{2,1,0:T(8,128)(2,1)} %refs_0_.1, s32[16,16]{1,0:T(8,128)} %refs_1_.1, ...), custom_call_target="tpu_custom_call" | custom-call | tf_op jit(solution)/shard_map/pallas_call | solution.py:481
  69.1 0.8 %shard_map.217 = (bf16[256,128]{1,0:T(8,128)(2,1)}, f32[256,128]{1,0:T(8,128)}, f32[16,128]{1,0:T(8,128)}, bf16[3,16,768]{2,1,0:T(8,128)(2,1)}, bf16[3,16,768]{2...) custom-call(bf16[256,128]{1,0:T(8,128)(2,1)S(1)} %get-tuple-element.20.refs_0_, ...), custom_call_target="tpu_custom_call" | custom-call | tf_op jit(solution)/shard_map/pallas_call | solution.py:531

commit v5 on v4

--- a/solution.py
+++ b/solution.py
@@ -146,10 +146,23 @@
         pltpu.make_async_copy(src, dst, sem_out.at[k])
         for k, (src, dst) in enumerate(zip(results, given, strict=True))
     ]
+    def to_plane(step):
+        return {"row": (row + step % 8) % 8, "col": zed * 4 + (ex + step // 8) % 4}
+
+    def to_depth(step):
+        return {"group": (group + step) % 2, "col": (zed + step // 2) % 4 * 4 + ex}
+
     barrier = pltpu.get_barrier_semaphore()
     for step in range(1, S):
         pl.semaphore_signal(barrier, inc=1, device_id=to_col(step), device_id_type=MESH)
         pl.semaphore_signal(barrier, inc=1, device_id=to_line(step), device_id_type=MESH)
+    greeted = 2 * (S - 1)
+    others = [to_plane(k) for k in range(9, 32) if k % 8]
+    others += [to_depth(k) for k in (3, 5, 7)]
+    others += [{"row": high * 2 + 1 - core, "col": col_at(d)} for d in range(4, S)]
+    for there in others:
+        pl.semaphore_signal(barrier, inc=1, device_id=there, device_id_type=MESH)
+    greeted += len(others)
 
     loads = [
         pltpu.make_async_copy(src, dst, sem_in.at[k])
@@ -171,7 +184,7 @@
     right = dot(pair_in, tri_proj[:, 2 * C : 4 * C])
     right = sigmoid(right[:, :C]) * right[:, C:] * mask_col
     r_send[...] = swap_blocks(right, 8).astype(BF16).reshape(S, S, C)
-    pl.semaphore_wait(barrier, 2 * (S - 1))
+    pl.semaphore_wait(barrier, greeted)
     for d in range(1, S):
         send(r_send.at[col_at(d)], r_own.at[col], ("r", d // 4), to_col(d))
     r_own[col] = r_send[col]
@@ -243,20 +256,10 @@
     def ag_key(dz, k):
         return ("ag", dz, k) if dz == 2 else ("ag", dz)
 
-    def fw_key(dz, k):
-        return ("fw", dz, k) if dz == 2 else ("fw", dz)
-
     def spread_right(dz):
         arrive(("r", dz), r_own.at[pl.ds(0, 4 if dz else 3)])
-        block = r_own.at[z_block(dz)]
-        there = r_all.at[mine, z_block(dz)]
         for k in range(1, 8):
-            send(block, there, ag_key(dz, k), to_quad(k))
-        send(block, there, fw_key(dz, 0), partner)
-
-    def relay(dz, k):
-        block = r_all.at[from_quad(k, core), z_block(dz)]
-        send(block, block, fw_key(dz, k), partner)
+            send(r_own.at[z_block(dz)], r_all.at[quad, z_block(dz)], ag_key(dz, k), to_quad(k))
 
     spread_right(0)
     spread_right(1)
@@ -266,34 +269,50 @@
     arrive("l", l_own.at[pl.ds(0, S - 1)])
     for d in range(1, 4):
         send(w_own.at[mine], w_rem.at[mine, d - 1], "w", {"col": (zed + 4 - d) % 4 * 4 + ex})
-    left_t[...] = l_own[...].reshape(N, C).astype(F32).T.astype(BF16)
-    diagonal = iota((C, C), 0) % 8 == iota((C, C), 1) % 8
+    left_t[core] = l_own[...].reshape(N, C).astype(F32).T.astype(BF16)
+    send(left_t.at[core], left_t.at[core], "lt", partner)
+    diagonal = iota((2 * C, C), 0) % 8 == iota((2 * C, C), 1) % 8
 
     def triangle(at, block):
-        product = dot(left_t[...], block.reshape(N, C))
-        product = jnp.where(diagonal, product, 0.0).reshape(S, 8, C)
-        t_send[at] = jnp.sum(product, axis=1).astype(BF16)
-
-    triangle(mine, r_own[...])
+        product = dot(left_t[...].reshape(2 * C, N), block.reshape(N, C))
+        product = jnp.where(diagonal, product, 0.0).reshape(2 * S, 8, C)
+        product = jnp.sum(product, axis=1).astype(BF16)
+        t_send[0, at] = product[:S]
+        t_send[1, at] = product[S:]
+
+    before_bias(2)
+    arrive("lt", left_t.at[0])
+    triangle(quad, r_own[...])
     for dz in (0, 1, 3):
         arrive(("ag", dz), r_all.at[pl.ds(0, 7), pl.ds(0, 4)])
-        for k in range(1, 8):
-            relay(dz, k)
-    before_bias(2)
     for k in range(1, 8):
         arrive(("ag", 2, k), r_all.at[0, pl.ds(0, 4)])
-        relay(2, k)
-        triangle(from_quad(k, core), r_all[from_quad(k, core)])
-    for dz in (0, 1, 3):
-        arrive(("fw", dz), r_all.at[pl.ds(0, 8), pl.ds(0, 4)])
-    for k in range(8):
-        arrive(("fw", 2, k), r_all.at[0, pl.ds(0, 4)])
-        triangle(from_quad(k, 1 - core), r_all[from_quad(k, 1 - core)])
-    for d in range(1, S):
-        send(t_send.at[col_at(d)], t_recv.at[col], "t", to_col(d))
-    t_recv[col] = t_send[col]
-
-    arrive("t", t_recv.at[pl.ds(0, S - 1)])
+        at = (quad + 8 - k) % 8
+        triangle(at, r_all[at])
+    same = col % 2 == core
+    for m in range(8):
+        at = (col // 2 + m) % 8
+        there = 2 * at + core
+        if m:
+            send(t_send.at[core, at], t_recv.at[col], "t", {"col": there})
+        send(
+            t_send.at[1 - core, at], t_recv.at[col], "t",
+            {"row": high * 2 + 1 - core, "col": there},
+        )
+    near = col // 2
+
+    @pl.when(same)
+    def _():
+        pltpu.make_async_copy(
+            t_send.at[core, near], t_recv.at[col], sems.at[1, keys["t"]]
+        ).start()
+
+    @pl.when(jnp.logical_not(same))
+    def _():
+        send(t_send.at[core, near], t_recv.at[col], "t", {"col": 2 * near + core})
+
+    arrive("t", t_recv)
+    bulks["t"] = t_recv.at[pl.ds(0, S - 1)]
     moved = swap_blocks(t_recv[...].astype(F32).reshape(N, C), 8)
     for j in range(S):
         row_scr[pl.ds(j, S, stride=S), :] = moved[j * S : (j + 1) * S]
@@ -425,9 +444,9 @@
     arrive("bb", bb_recv.at[pl.ds(0, S - 1)])
     grad_bias = jnp.concatenate([bb_recv[k] for k in range(S)], axis=0).astype(BF16)
     ar_one[...] = dot(grad_bias, bias_in_scr[...]).astype(BF16)
-    for d in range(1, S):
-        send(ar_one, ar_all.at[mine], "a1", to_line(d))
-    ar_all[mine] = ar_one[...]
+    for k in range(1, 32):
+        send(ar_one, ar_all.at[row * 4 + ex], "a1", to_plane(k))
+    ar_all[row * 4 + ex] = ar_one[...]
     grad_in = dot_tn(grad_bias, bw_pad[:S, :])
     pair_grad[...] = norm_back(grad_in, upd_scr[...], bias_gain[...])
     stores[1].start()
@@ -436,11 +455,11 @@
     ws_recv[quad] = ws_sum[quad]
     project(1)
     project(2)
-    arrive("a1", ar_all.at[pl.ds(0, S - 1)])
+    arrive("a1", ar_all.at[pl.ds(0, 31)])
     ar_two[...] = jnp.sum(ar_all[...].astype(F32), axis=0).astype(BF16)
-    for d in range(1, S):
-        send(ar_two, ar_fin.at[col], "a2", to_col(d))
-    ar_fin[col] = ar_two[...]
+    for k in range(1, 8):
+        send(ar_two, ar_fin.at[group * 4 + zed], "a2", to_depth(k))
+    ar_fin[group * 4 + zed] = ar_two[...]
     finish(0)
     finish(1)
     finish(2)
@@ -449,9 +468,14 @@
     arrive("ws", ws_recv.at[pl.ds(0, 7)])
     weight_grad[...] = jnp.sum(ws_recv[...].astype(F32), axis=0)
     stores[5].start()
-    arrive("a2", ar_fin.at[pl.ds(0, S - 1)])
+    arrive("a2", ar_fin.at[pl.ds(0, 7)])
     bias_weight_grad[...] = jnp.sum(ar_fin[...].astype(F32), axis=0)
     stores[2].start()
+    @pl.when(jnp.logical_not(same))
+    def _():
+        extra = t_recv.at[0]
+        pltpu.make_async_copy(extra, extra, sems.at[0, keys["t"]]).wait()
+
     for key, bulk in bulks.items():
         pltpu.make_async_copy(bulk, bulk, sems.at[0, keys[key]]).wait()
     for copy in stores:
@@ -498,9 +522,9 @@
             pltpu.SemaphoreType.DMA((17,)),
             buf(N, C, kind=F32),
             buf(S, S, C), buf(S, S, C), buf(S, S, C), buf(S, S, C),
-            buf(S, S, S, C),
-            buf(C, N),
-            buf(S, S, C), buf(S, S, C),
+            buf(8, S, S, C),
+            buf(2, C, N),
+            buf(2, 8, S, C), buf(S, S, C),
             buf(N, C, kind=F32), buf(N, C, kind=F32),
             buf(N, C), buf(C, C),
             buf(S, 1, N, kind=F32), buf(S, 1, N, kind=F32), buf(S, S, N),
@@ -514,8 +538,8 @@
             buf(S, S, N), buf(S, S, N),
             buf(S, 1, N, kind=F32), buf(S, 1, N, kind=F32),
             buf(2, 8, E, N), buf(8, E, N), buf(8, E, N), buf(8, E, N),
-            buf(S, C), buf(S, S, C), buf(S, C), buf(S, S, C),
-            pltpu.SemaphoreType.DMA((2, 45)),
+            buf(S, C), buf(32, S, C), buf(S, C), buf(8, S, C),
+            pltpu.SemaphoreType.DMA((2, 35)),
             buf(N, C), buf(N, C, kind=F32), buf(S, C, kind=F32), buf(T, S, D), buf(T, S, D),
             buf(E, N, kind=F32), pltpu.SemaphoreType.DMA((6,)),
         ],

time: 70 us -> 68.8 us (0.983)
  Pallas kernels: 69.2 us -> 68.1 us
    pallas_call x1, Pallas kernels: 68.4 us -> 67.3 us  [shards(): pl.pallas_call(kernel, out_shape=(jax.ShapeDtypeStruct((N, C), BF16), jax...]
where the time goes in v5:
time: 68.8 us; the launch traced here: 68.7 us
  Pallas kernels  68.1 us (99%)
    pallas_call x1, Pallas kernels, shards(): pl.pallas_call(kernel, out_shape=(jax.ShapeDtypeStruct((N, C), BF16), jax...  67.3 us

profile of v5, /device:TPU:1, one launch (start us, length us, event | category | flops | bytes accessed | tf_op | source)
XLA Modules:
  0.0 68.7 jit_solution(311233090208207765)
XLA Ops:
  0.6 67.3 %shard_map.216 = (bf16[256,128]{1,0:T(8,128)(2,1)S(1)}, f32[256,128]{1,0:T(8,128)S(1)}, f32[16,128]{1,0:T(8,128)S(1)}, bf16[3,16,768]{2,1,0:T(8,128)(2,1)S(1)}, ...) custom-call(bf16[16,16,128]{2,1,0:T(8,128)(2,1)} %refs_0_.1, s32[16,16]{1,0:T(8,128)} %refs_1_.1, ...), custom_call_target="tpu_custom_call" | custom-call | tf_op jit(solution)/shard_map/pallas_call | solution.py:505
  68.0 0.8 %shard_map.217 = (bf16[256,128]{1,0:T(8,128)(2,1)}, f32[256,128]{1,0:T(8,128)}, f32[16,128]{1,0:T(8,128)}, bf16[3,16,768]{2,1,0:T(8,128)(2,1)}, bf16[3,16,768]{2...) custom-call(bf16[256,128]{1,0:T(8,128)(2,1)S(1)} %get-tuple-element.20.refs_0_, ...), custom_call_target="tpu_custom_call" | custom-call | tf_op jit(solution)/shard_map/pallas_call | solution.py:555

commit v6 on v5

--- a/solution.py
+++ b/solution.py
@@ -311,6 +311,14 @@
     def _():
         send(t_send.at[core, near], t_recv.at[col], "t", {"col": 2 * near + core})
 
+    def to_high(k):
+        return {"row": (high + k) % 4 * 2 + core}
+
+    arrive("w", w_rem.at[0])
+    send(w_rem.at[mine], w_rem.at[mine], "wz", {"group": 1 - group})
+    for k in range(1, 4):
+        send(w_rem.at[mine], w_rem.at[mine], "wy", to_high(k))
+    send(w_rem.at[mine], w_rem.at[mine], "wf", partner)
     arrive("t", t_recv)
     bulks["t"] = t_recv.at[pl.ds(0, S - 1)]
     moved = swap_blocks(t_recv[...].astype(F32).reshape(N, C), 8)
@@ -341,10 +349,10 @@
         b_send[k] = by_head[k : k + 1]
     for d in range(1, S):
         send(b_send.at[col_at(d)], b_recv.at[col], "b", to_col(d))
-    arrive("w", w_rem.at[0])
-    for k in range(1, 8):
-        send(w_rem.at[mine], w_rem.at[mine], "wg", to_quad(k))
-    send(w_rem.at[mine], w_rem.at[mine], "wf", partner)
+    arrive("wz", w_rem.at[0])
+    beside = (1 - group) * 8 + row
+    for k in range(1, 4):
+        send(w_rem.at[beside], w_rem.at[beside], "wyz", to_high(k))
     b_recv[col] = b_send[col]
     pair_next[...] = updated.astype(BF16)
     stores[0].start()
@@ -393,7 +401,8 @@
     for k in range(S):
         ws_send[k % 2, k // 2] = turned[k * E : (k + 1) * E].astype(BF16)
     send(ws_send.at[1 - core], ws_half, "wh", partner)
-    arrive("wg", w_rem.at[pl.ds(0, 7)])
+    arrive("wy", w_rem.at[pl.ds(0, 3)])
+    arrive("wyz", w_rem.at[pl.ds(0, 3)])
     for k in range(1, 8):
         at = from_quad(k, core)
         send(w_rem.at[at], w_rem.at[at], "wf", partner)
@@ -539,7 +548,7 @@
             buf(S, 1, N, kind=F32), buf(S, 1, N, kind=F32),
             buf(2, 8, E, N), buf(8, E, N), buf(8, E, N), buf(8, E, N),
             buf(S, C), buf(32, S, C), buf(S, C), buf(8, S, C),
-            pltpu.SemaphoreType.DMA((2, 35)),
+            pltpu.SemaphoreType.DMA((2, 37)),
             buf(N, C), buf(N, C, kind=F32), buf(S, C, kind=F32), buf(T, S, D), buf(T, S, D),
             buf(E, N, kind=F32), pltpu.SemaphoreType.DMA((6,)),
         ],

time: 68.8 us -> 68 us (0.988)
  Pallas kernels: 68.1 us -> 67.2 us
    pallas_call x1, Pallas kernels: 67.3 us -> 66.4 us  [shards(): pl.pallas_call(kernel, out_shape=(jax.ShapeDtypeStruct((N, C), BF16), jax...]
where the time goes in v6:
time: 68 us; the launch traced here: 67.9 us
  Pallas kernels  67.2 us (99%)
    pallas_call x1, Pallas kernels, shards(): pl.pallas_call(kernel, out_shape=(jax.ShapeDtypeStruct((N, C), BF16), jax...  66.4 us

profile of v6, /device:TPU:1, one launch (start us, length us, event | category | flops | bytes accessed | tf_op | source)
XLA Modules:
  0.0 67.9 jit_solution(11197704160965910592)
XLA Ops:
  0.6 66.4 %shard_map.216 = (bf16[256,128]{1,0:T(8,128)(2,1)S(1)}, f32[256,128]{1,0:T(8,128)S(1)}, f32[16,128]{1,0:T(8,128)S(1)}, bf16[3,16,768]{2,1,0:T(8,128)(2,1)S(1)}, ...) custom-call(bf16[16,16,128]{2,1,0:T(8,128)(2,1)} %refs_0_.1, s32[16,16]{1,0:T(8,128)} %refs_1_.1, ...), custom_call_target="tpu_custom_call" | custom-call | tf_op jit(solution)/shard_map/pallas_call | solution.py:514
  67.1 0.8 %shard_map.217 = (bf16[256,128]{1,0:T(8,128)(2,1)}, f32[256,128]{1,0:T(8,128)}, f32[16,128]{1,0:T(8,128)}, bf16[3,16,768]{2,1,0:T(8,128)(2,1)}, bf16[3,16,768]{2...) custom-call(bf16[256,128]{1,0:T(8,128)(2,1)S(1)} %get-tuple-element.20.refs_0_, ...), custom_call_target="tpu_custom_call" | custom-call | tf_op jit(solution)/shard_map/pallas_call | solution.py:564

commit v7 on v6

--- a/solution.py
+++ b/solution.py
@@ -184,13 +184,13 @@
     right = dot(pair_in, tri_proj[:, 2 * C : 4 * C])
     right = sigmoid(right[:, :C]) * right[:, C:] * mask_col
     r_send[...] = swap_blocks(right, 8).astype(BF16).reshape(S, S, C)
+    left = dot(pair_in, tri_proj[:, : 2 * C])
+    left = sigmoid(left[:, :C]) * left[:, C:] * mask_col
+    l_send[...] = swap_blocks(left, 8).astype(BF16).reshape(S, S, C)
     pl.semaphore_wait(barrier, greeted)
     for d in range(1, S):
         send(r_send.at[col_at(d)], r_own.at[col], ("r", d // 4), to_col(d))
     r_own[col] = r_send[col]
-    left = dot(pair_in, tri_proj[:, : 2 * C])
-    left = sigmoid(left[:, :C]) * left[:, C:] * mask_col
-    l_send[...] = swap_blocks(left, 8).astype(BF16).reshape(S, S, C)
     for d in range(1, S):
         send(l_send.at[col_at(d)], l_own.at[col], "l", to_col(d))
     l_own[col] = l_send[col]
@@ -363,6 +363,11 @@
         send(b_all.at[mine], b_all.at[mine], "ba", to_line(d))
     arrive("ba", b_all.at[pl.ds(0, S - 1)])
 
+    arrive("wy", w_rem.at[pl.ds(0, 3)])
+    arrive("wyz", w_rem.at[pl.ds(0, 3)])
+    for k in range(1, 8):
+        at = from_quad(k, core)
+        send(w_rem.at[at], w_rem.at[at], "wf", partner)
     bias = b_all[...].reshape(N, N).astype(F32)
     copies = range(T)
     exponent = [jnp.exp(score_scr[t] + bias) for t in copies]
@@ -401,11 +406,6 @@
     for k in range(S):
         ws_send[k % 2, k // 2] = turned[k * E : (k + 1) * E].astype(BF16)
     send(ws_send.at[1 - core], ws_half, "wh", partner)
-    arrive("wy", w_rem.at[pl.ds(0, 3)])
-    arrive("wyz", w_rem.at[pl.ds(0, 3)])
-    for k in range(1, 8):
-        at = from_quad(k, core)
-        send(w_rem.at[at], w_rem.at[at], "wf", partner)
     def project(t):
         arrive(("z", t), raw_z.at[t])
         total = jnp.zeros((C, D), F32)

time: 68 us -> 66.7 us (0.981)
  Pallas kernels: 67.2 us -> 65.9 us
    pallas_call x1, Pallas kernels: 66.4 us -> 65.1 us  [shards(): pl.pallas_call(kernel, out_shape=(jax.ShapeDtypeStruct((N, C), BF16), jax...]
where the time goes in v7:
time: 66.7 us; the launch traced here: 66.6 us
  Pallas kernels  65.9 us (99%)
    pallas_call x1, Pallas kernels, shards(): pl.pallas_call(kernel, out_shape=(jax.ShapeDtypeStruct((N, C), BF16), jax...  65.1 us

profile of v7, /device:TPU:1, one launch (start us, length us, event | category | flops | bytes accessed | tf_op | source)
XLA Modules:
  0.0 66.6 jit_solution(16317461233540994668)
XLA Ops:
  0.6 65.1 %shard_map.216 = (bf16[256,128]{1,0:T(8,128)(2,1)S(1)}, f32[256,128]{1,0:T(8,128)S(1)}, f32[16,128]{1,0:T(8,128)S(1)}, bf16[3,16,768]{2,1,0:T(8,128)(2,1)S(1)}, ...) custom-call(bf16[16,16,128]{2,1,0:T(8,128)(2,1)} %refs_0_.1, s32[16,16]{1,0:T(8,128)} %refs_1_.1, ...), custom_call_target="tpu_custom_call" | custom-call | tf_op jit(solution)/shard_map/pallas_call | solution.py:514
  65.8 0.8 %shard_map.217 = (bf16[256,128]{1,0:T(8,128)(2,1)}, f32[256,128]{1,0:T(8,128)}, f32[16,128]{1,0:T(8,128)}, bf16[3,16,768]{2,1,0:T(8,128)(2,1)}, bf16[3,16,768]{2...) custom-call(bf16[256,128]{1,0:T(8,128)(2,1)S(1)} %get-tuple-element.20.refs_0_, ...), custom_call_target="tpu_custom_call" | custom-call | tf_op jit(solution)/shard_map/pallas_call | solution.py:564
